TPU v7x, 512 devices: a 4x2x32 block of a 4x16x32 slice. The times are simulated.
512 devices in a mesh: dom: 2 (over y), grid: 32 (over z), band: 4 (over x), mem: 2 (over core).
Axes of the slice: x: 4, y: 2, z: 32, core: 2. Of those that a mesh axis runs over, the one named last changes fastest.
The devices are a block of a 4x16x32 slice.
Arguments:
- grid_state: bfloat16 [4, 16384, 128], P(('dom', 'mem'), 'grid'), parts along dimension 0, may hold values from -6 to 6
- forcing: bfloat16 [32768, 128], P(('dom', 'grid')), parts along dimension 0, may hold values from -6 to 6
- boundary_mask: int32 [16384], P('grid'), may hold values 0 or 1
- edge_src: int32 [32, 32, 32], P('grid'), may hold values from 0 to 511
- edge_dst: int32 [32, 32, 32], P(None, 'grid'), may hold values from 0 to 127
- edge_count: int32 [32, 32], P(None, 'grid'), may hold values from 0 to 32, as said below
- edge_weight: float32 [32, 32, 32], P(None, 'grid'), may hold values from 0.1 to 1
- embed_weight: bfloat16 [128, 1024], P(None, 'band'), may hold values from -0.5 to 0.5
- attn_qkv: bfloat16 [1, 1024, 3, 1024], P(None, 'mem', None, 'band'), may hold values from -0.1875 to 0.1875
- attn_out: bfloat16 [1, 1024, 1024], P(None, 'band', 'mem'), may hold values from -0.1875 to 0.1875
- mlp_in: bfloat16 [1, 1024, 4096], P(None, 'mem', 'band'), may hold values from -0.1875 to 0.1875
- mlp_out: bfloat16 [1, 4096, 1024], P(None, 'band', 'mem'), may hold values from -0.09375 to 0.09375
- decode_weight: bfloat16 [1024, 128], P('band'), may hold values from -0.1875 to 0.1875
Outputs:
- next_state: bfloat16 [4, 16384, 128], P(('dom', 'mem'), 'grid'), parts along dimension 0
There are 2 independent parts, one for each index of `dom`. A program takes and returns all parts, laid end to end along the dimension named above; an argument that names none is the same for every part. Nothing has to cross between parts.
Inputs may be any that keep to these rules, and one draw needn't show every extreme that they name: Slots at or beyond edge_count[i, j] in a block are padding. In every draw some mesh band receives 32 live slots from every grid shard.
All inputs are finite; a program needn't handle non-finite values. No bound on the sum of `boundary_mask` on one device may be relied on, other than what follows from the above.
Results may differ from a plain program's by a relative error of at most 0.011.
Values may be sent and summed in bfloat16 or wider, within the bound.
A program may use at most 64 MiB of HBM per device.

v0:
```python
import jax
import jax.numpy as jnp
from jax import lax
from jax.sharding import PartitionSpec as P

HEADS = 16
GP_DEV = 512
M_DEV = 128
WINDOW = 64


def copy_for_each(shard, axis):
    copies = jnp.broadcast_to(shard, (lax.axis_size(axis), *shard.shape))
    return lax.all_to_all(copies, axis, split_axis=0, concat_axis=0, tiled=True)


def joined_along(parts, dim):
    parts = jnp.moveaxis(parts, 0, dim)
    shape = parts.shape
    return parts.reshape(*shape[:dim], shape[dim] * shape[dim + 1], *shape[dim + 2 :])


def gathered_copies(shard, axis, dim):
    parts = copy_for_each(shard, axis)
    return joined_along(parts, dim)


def rows_first(arrays, axis, dims):
    turned = [jnp.moveaxis(a, dim, 0) for a, dim in zip(arrays, dims)]
    widths = [t[0].size for t in turned]
    both = jnp.concatenate([t.reshape(-1, w) for t, w in zip(turned, widths)], axis=1)
    whole = lax.all_gather(both, axis, axis=0, tiled=True)
    parts = jnp.split(whole, [sum(widths[:k]) for k in range(1, len(widths))], axis=1)
    return tuple(
        (
            jnp.moveaxis(b.reshape(-1, *t.shape[1:]), 0, dim)
            for b, t, dim in zip(parts, turned, dims)
        )
    )


def extended(block, sides, width):
    for axis, dim in sides:
        count = lax.axis_size(axis)
        forward = [(i, i + 1) for i in range(count - 1)]
        backward = [(target, source) for source, target in forward]
        low = lax.ppermute(
            lax.slice_in_dim(block, block.shape[dim] - width, None, axis=dim), axis, forward
        )
        high = lax.ppermute(lax.slice_in_dim(block, 0, width, axis=dim), axis, backward)
        block = jnp.concatenate([low, block, high], axis=dim)
    return block


def taken_together(shard, axis):
    everything = copy_for_each(shard, axis)
    return jnp.sum(everything.astype(jnp.float32), axis=0)


def cut_along(shard, dim, count):
    before, after = (shard.shape[:dim], shard.shape[dim + 1 :])
    return jnp.moveaxis(shard.reshape(*before, count, -1, *after), dim, 0)


def summed_on_arrival(shard, axis, dim):
    parts = cut_along(shard, dim, lax.axis_size(axis))
    arrived = lax.all_to_all(parts, axis, split_axis=0, concat_axis=0, tiled=True)
    return arrived.astype(jnp.float32).sum(axis=0)


def rms_norm(values):
    return values * lax.rsqrt(jnp.mean(values * values, axis=-1, keepdims=True) + 1e-06)


def body(
    grid_state,
    forcing,
    boundary_mask,
    edge_src,
    edge_dst,
    edge_count,
    edge_weight,
    embed_weight,
    attn_qkv,
    attn_out,
    mlp_in,
    mlp_out,
    decode_weight,
):
    shards = lax.axis_size("grid")
    grid_index = lax.axis_index("grid")
    col_width = embed_weight.shape[1]
    grid_rows = grid_state[0]
    var_count = grid_rows.shape[1]
    slot_count = edge_dst.shape[2]
    sources = edge_src[0].reshape(-1)
    targets = edge_dst[:, 0].reshape(-1)
    live_slot = jnp.arange(slot_count, dtype=jnp.int32)[None, :] < edge_count[:, 0][:, None]
    weights = jnp.where(live_slot, edge_weight[:, 0], 0.0).reshape(-1)
    picked = grid_rows[sources].reshape(shards, slot_count, var_count)
    arrived = lax.all_to_all(picked, "grid", split_axis=0, concat_axis=0, tiled=True)
    latent = jax.nn.gelu(
        jnp.dot(arrived.reshape(-1, var_count), embed_weight, preferred_element_type=jnp.float32)
    )
    mesh_part = jax.ops.segment_sum(latent * weights[:, None], targets, num_segments=M_DEV)
    mesh_in = gathered_copies(mesh_part.astype(jnp.bfloat16), "band", 1)
    stream = mesh_in.astype(jnp.float32)
    mesh_rows = stream.shape[0]
    model_width = stream.shape[1]
    head_dim = model_width // HEADS
    local_heads = col_width // head_dim
    query_pos = grid_index * mesh_rows + jnp.arange(mesh_rows, dtype=jnp.int32)
    key_pos = grid_index * mesh_rows - WINDOW + jnp.arange(mesh_rows + 2 * WINDOW, dtype=jnp.int32)
    visible = (
        (jnp.abs(query_pos[:, None] - key_pos[None, :]) <= WINDOW)
        & (key_pos[None, :] >= 0)
        & (key_pos[None, :] < mesh_rows * shards)
    )
    w_qkv, w_out, w_in, w_back = rows_first(
        (attn_qkv[0], attn_out[0], mlp_in[0], mlp_out[0]), "mem", (0, 1, 0, 1)
    )
    normed = rms_norm(stream).astype(jnp.bfloat16)
    mixed_qkv = jnp.dot(
        normed, w_qkv.reshape(model_width, 3 * col_width), preferred_element_type=jnp.float32
    )
    mixed_qkv = mixed_qkv.reshape(mesh_rows, 3, local_heads, head_dim)
    queries = rms_norm(mixed_qkv[:, 0]).astype(jnp.bfloat16)
    keys_now = rms_norm(mixed_qkv[:, 1]).astype(jnp.bfloat16).reshape(mesh_rows, col_width)
    values = mixed_qkv[:, 2].astype(jnp.bfloat16).reshape(mesh_rows, col_width)
    padded = extended(jnp.stack([keys_now, values]), (("grid", 1),), WINDOW)
    near_keys = padded[0].reshape(-1, local_heads, head_dim)
    near_values = padded[1].reshape(-1, local_heads, head_dim)
    scores = jnp.einsum(
        "qhd,khd->hqk", queries, near_keys, preferred_element_type=jnp.float32
    ) * head_dim ** (-0.5)
    exp_scores = jnp.where(visible[None], jnp.exp(scores), 0.0)
    shares = (exp_scores / jnp.sum(exp_scores, axis=-1, keepdims=True)).astype(jnp.bfloat16)
    attended = jnp.einsum("hqk,khd->qhd", shares, near_values, preferred_element_type=jnp.float32)
    attended = attended.astype(jnp.bfloat16).reshape(mesh_rows, col_width)
    stream = stream + taken_together(
        jnp.dot(attended, w_out, preferred_element_type=jnp.float32).astype(jnp.bfloat16), "band"
    ).astype(jnp.float32)
    normed = rms_norm(stream).astype(jnp.bfloat16)
    hidden = jax.nn.gelu(jnp.dot(normed, w_in, preferred_element_type=jnp.float32)).astype(
        jnp.bfloat16
    )
    stream = stream + taken_together(
        jnp.dot(hidden, w_back, preferred_element_type=jnp.float32).astype(jnp.bfloat16), "band"
    ).astype(jnp.float32)
    mesh_out = stream.astype(jnp.bfloat16)
    mesh_cols = lax.dynamic_slice_in_dim(mesh_out, lax.axis_index("band") * col_width, col_width, 1)
    proj_part = summed_on_arrival(
        jnp.dot(mesh_cols, decode_weight, preferred_element_type=jnp.float32).astype(jnp.bfloat16),
        "band",
        1,
    )
    part_width = proj_part.shape[1]
    outgoing = (proj_part[targets] * weights[:, None]).reshape(shards, slot_count, part_width)
    returned = lax.all_to_all(
        outgoing.astype(jnp.bfloat16), "grid", split_axis=0, concat_axis=0, tiled=True
    ).astype(outgoing.dtype)
    decoded_part = jax.ops.segment_sum(
        returned.reshape(-1, part_width), sources, num_segments=GP_DEV
    )
    decoded = gathered_copies(decoded_part.astype(jnp.bfloat16), "band", 1).astype(
        decoded_part.dtype
    )
    forced = boundary_mask[:, None] == 1
    result = jnp.where(forced, forcing.astype(jnp.float32), grid_rows.astype(jnp.float32) + decoded)
    return result.astype(jnp.bfloat16)[None]


def solution(mesh):
    return jax.shard_map(
        body,
        mesh=mesh,
        in_specs=(
            P(("dom", "mem"), "grid", None),
            P(("dom", "grid"), None),
            P("grid"),
            P("grid", None, None),
            P(None, "grid", None),
            P(None, "grid"),
            P(None, "grid", None),
            P(None, "band"),
            P(None, "mem", None, "band"),
            P(None, "band", "mem"),
            P(None, "mem", "band"),
            P(None, "band", "mem"),
            P("band", None),
        ),
        out_specs=P(("dom", "mem"), "grid", None),
        check_vma=False,
    )
```

profile of v0, /device:TPU:40, one launch (start us, length us, event | category | flops | bytes accessed | tf_op | source)
XLA Modules:
  0.0 242.3 jit_solution(12147765674449704276)
XLA Ops:
  6.6 1.6 copy.47
  8.2 1.4 copy.46
  9.6 1.8 pad_maximum_fusion
  12.3 4.3 %gather_fusion = bf16[1024,128]{1,0:T(8,128)(2,1)} fusion(bf16[512,128]{1,0:T(8,128)(2,1)S(1)} %bitcast.78, s32[1024]{0:T(1024)S(1)} %broadcast_clamp_fusion.1), kind=kCustom, calls=%fused_computation | custom fusion | bytes 528384 | tf_op jit(solution)/shard_map/gather | solution.py:100
  16.6 45.8 %all-to-all-start = ((bf16[32,32,128]{2,1,0:T(8,128)(2,1)}), bf16[32,32,128]{2,1,0:T(8,128)(2,1)S(1)}, u32[]{:S(2)}, u32[]{:S(2)}) async-start(bf16[32,32,128]{2,1,0:T(8,128)(2,1)} %bitcast.2), calls=%async_computation | async-start | bytes 524288 | tf_op jit(solution)/shard_map/all_to_all | solution.py:101
  65.2 39.1 %all-to-all-done = bf16[32,32,128]{2,1,0:T(8,128)(2,1)S(1)} async-done(((bf16[32,32,128]{2,1,0:T(8,128)(2,1)}), bf16[32,32,128]{2,1,0:T(8,128)(2,1)S(1)}, u32[]{:S(2)}, u32[]{:S(2)}) %all-to-all-start) | async-done | bytes 262176 | tf_op jit(solution)/shard_map/all_to_all | solution.py:101
  104.8 6.1 %scatter_custom_fusion = f32[128,256]{1,0:T(8,128)S(1)} fusion(s32[1024]{0:T(1024)S(1)} %reshape.288, f32[1024,256]{1,0:T(8,128)S(1)} %fusion.16, f32[]{:T(128)} %constant.22.clone.1), kind=kCustom, calls=%fused_computation.75 | custom fusion | flops 262144 | bytes 131076 | tf_op jit(solution)/shard_map/scatter-add | solution.py:105
  111.6 4.6 %all-to-all-start.1 = ((bf16[4,128,256]{2,1,0:T(8,128)(2,1)}), bf16[4,128,256]{2,1,0:T(8,128)(2,1)S(1)}, u32[]{:S(2)}, u32[]{:S(2)}) async-start(bf16[4,128,256]{2,1,0:T(8,128)(2,1)} %broadcast_in_dim.65), calls=%async_computation.1 | async-start | bytes 524288 | tf_op jit(solution)/shard_map/all_to_all | solution.py:14
  116.3 6.6 %all-to-all-done.1 = bf16[4,128,256]{2,1,0:T(8,128)(2,1)S(1)} async-done(((bf16[4,128,256]{2,1,0:T(8,128)(2,1)}), bf16[4,128,256]{2,1,0:T(8,128)(2,1)S(1)}, u32[]{:S(2)}, u32[]{:S(2)}) %all-to-all-start.1) | async-done | bytes 262176 | tf_op jit(solution)/shard_map/all_to_all | solution.py:14
  126.9 4.6 %collective-permute-start = (bf16[2,64,256]{1,2,0:T(8,128)(2,1)S(1)}, bf16[2,64,256]{1,2,0:T(8,128)(2,1)S(1)}, u32[]{:S(2)}, u32[]{:S(2)}) collective-permute-start(bf16[2,64,256]{1,2,0:T(8,128)(2,1)S(1)} %get-tuple-element.9), channel_id=1, source_target_pairs={{0,8},{8,16},{16,24},{24,32},{32,40},{40,48},{48,56},{56,64},{64,7... | collective-permute-start | bytes 196616 | tf_op jit(solution)/shard_map/ppermute | solution.py:47
  132.4 1.5 collective-permute-done
  137.2 3.6 %all-to-all-start.2 = ((bf16[4,128,1024]{2,1,0:T(8,128)(2,1)}), bf16[4,128,1024]{2,1,0:T(8,128)(2,1)S(1)}, u32[]{:S(2)}, u32[]{:S(2)}) async-start(bf16[4,128,1024]{2,1,0:T(8,128)(2,1)} %broadcast_in_dim.68), calls=%async_computation.2 | async-start | bytes 2097152 | tf_op jit(solution)/shard_map/all_to_all | solution.py:14
  141.1 11.3 %all-to-all-done.2 = bf16[4,128,1024]{2,1,0:T(8,128)(2,1)S(1)} async-done(((bf16[4,128,1024]{2,1,0:T(8,128)(2,1)}), bf16[4,128,1024]{2,1,0:T(8,128)(2,1)S(1)}, u32[]{:S(2)}, u32[]{:S(2)}) %all-to-all-start.2) | async-done | bytes 1048608 | tf_op jit(solution)/shard_map/all_to_all | solution.py:14
  153.0 3.5 %fusion.6 = bf16[128,1024]{1,0:T(8,128)(2,1)S(1)} fusion(bf16[1024,3072]{0,1:T(8,128)(2,1)} %all-gather.2.cloned.1.call-done, f32[128,1024]{1,0:T(8,128)S(1)} %add.134, f32[128]{0:T(128)S(1)} %add_rsqrt_fusion.2), kind=kOutput, calls=%fused_computation.15 | convolution fusion | flops 538443776 | bytes 4981248 | tf_op jit(solution)/shard_map/dot_general | solution.py:148
  157.6 3.6 %all-to-all-start.3 = ((bf16[4,128,1024]{2,1,0:T(8,128)(2,1)}), bf16[4,128,1024]{2,1,0:T(8,128)(2,1)S(1)}, u32[]{:S(2)}, u32[]{:S(2)}) async-start(bf16[4,128,1024]{2,1,0:T(8,128)(2,1)} %broadcast_in_dim.69), calls=%async_computation.3 | async-start | bytes 2097152 | tf_op jit(solution)/shard_map/all_to_all | solution.py:14
  161.4 10.6 %all-to-all-done.3 = bf16[4,128,1024]{2,1,0:T(8,128)(2,1)S(1)} async-done(((bf16[4,128,1024]{2,1,0:T(8,128)(2,1)}), bf16[4,128,1024]{2,1,0:T(8,128)(2,1)S(1)}, u32[]{:S(2)}, u32[]{:S(2)}) %all-to-all-start.3) | async-done | bytes 1048608 | tf_op jit(solution)/shard_map/all_to_all | solution.py:14
  173.0 3.4 %all-to-all-start.4 = ((bf16[4,128,32]{1,2,0:T(8,128)(2,1)}), bf16[4,128,32]{1,2,0:T(8,128)(2,1)S(1)}, u32[]{:S(2)}, u32[]{:S(2)}) async-start(bf16[4,128,32]{1,2,0:T(8,128)(2,1)} %bitcast.27), calls=%async_computation.4 | async-start | bytes 65536 | tf_op jit(solution)/shard_map/all_to_all | solution.py:67
  176.4 5.3 %all-to-all-done.4 = bf16[4,128,32]{1,2,0:T(8,128)(2,1)S(1)} async-done(((bf16[4,128,32]{1,2,0:T(8,128)(2,1)}), bf16[4,128,32]{1,2,0:T(8,128)(2,1)S(1)}, u32[]{:S(2)}, u32[]{:S(2)}) %all-to-all-start.4) | async-done | bytes 32800 | tf_op jit(solution)/shard_map/all_to_all | solution.py:67
  181.9 2.8 %gather_fusion.1 = f32[1024,32]{1,0:T(8,128)S(1)} fusion(f32[128,32]{1,0:T(8,128)S(1)} %copy.51, s32[1024]{0:T(1024)S(1)} %broadcast_clamp_fusion), kind=kCustom, calls=%fused_computation.1 | custom fusion | bytes 266240 | tf_op jit(solution)/shard_map/gather | solution.py:158
  185.8 8.7 %all-to-all-start.5 = ((bf16[32,2,512]{2,1,0:T(2,128)(2,1)}), bf16[32,2,512]{2,1,0:T(2,128)(2,1)S(1)}, u32[]{:S(2)}, u32[]{:S(2)}) async-start(bf16[32,2,512]{2,1,0:T(2,128)(2,1)} %reshape.330), calls=%async_computation.5 | async-start | bytes 131072 | tf_op jit(solution)/shard_map/all_to_all | solution.py:159
  194.5 23.6 %all-to-all-done.5 = bf16[32,2,512]{2,1,0:T(2,128)(2,1)S(1)} async-done(((bf16[32,2,512]{2,1,0:T(2,128)(2,1)}), bf16[32,2,512]{2,1,0:T(2,128)(2,1)S(1)}, u32[]{:S(2)}, u32[]{:S(2)}) %all-to-all-start.5) | async-done | bytes 65568 | tf_op jit(solution)/shard_map/all_to_all | solution.py:159
  218.3 6.1 %scatter_custom_fusion.1 = f32[512,32]{1,0:T(8,128)S(1)} fusion(s32[1024]{0:T(1024)S(1)} %reshape.296, bf16[1024,32]{1,0:T(8,128)(2,1)S(1)} %bitcast.85, f32[]{:T(128)} %constant.22.clone.1), kind=kCustom, calls=%fused_computation.37 | custom fusion | flops 65536 | bytes 327684 | tf_op jit(solution)/shard_map/scatter-add | solution.py:162
  225.2 3.4 %all-to-all-start.6 = ((bf16[4,512,32]{1,2,0:T(8,128)(2,1)}), bf16[4,512,32]{1,2,0:T(8,128)(2,1)S(1)}, u32[]{:S(2)}, u32[]{:S(2)}) async-start(bf16[4,512,32]{1,2,0:T(8,128)(2,1)} %broadcast_in_dim.71), calls=%async_computation.6 | async-start | bytes 262144 | tf_op jit(solution)/shard_map/all_to_all | solution.py:14
  228.6 5.9 %all-to-all-done.6 = bf16[4,512,32]{1,2,0:T(8,128)(2,1)S(1)} async-done(((bf16[4,512,32]{1,2,0:T(8,128)(2,1)}), bf16[4,512,32]{1,2,0:T(8,128)(2,1)S(1)}, u32[]{:S(2)}, u32[]{:S(2)}) %all-to-all-start.6) | async-done | bytes 131104 | tf_op jit(solution)/shard_map/all_to_all | solution.py:14
  (92 shorter events, 19.3 us)
Async XLA Ops:
  6.5 97.8 %copy-start = (bf16[128,256]{1,0:T(8,128)(2,1)S(1)}, bf16[128,256]{1,0:T(8,128)(2,1)}, u32[]{:S(2)}) copy-start(bf16[128,256]{1,0:T(8,128)(2,1)} %param.20) | copy-start | bytes 196612
  6.6 3.0 %copy-start.2 = (bf16[1,1024,512]{2,1,0:T(8,128)(2,1)S(1)}, bf16[1,1024,512]{2,1,0:T(8,128)(2,1)}, u32[]{:S(2)}) copy-start(bf16[1,1024,512]{2,1,0:T(8,128)(2,1)} %param.24) | copy-start | bytes 3145732
  6.6 3.0 %copy-start.3 = (bf16[1,256,512]{2,1,0:T(8,128)(2,1)S(1)}, bf16[1,256,512]{2,1,0:T(8,128)(2,1)}, u32[]{:S(2)}) copy-start(bf16[1,256,512]{2,1,0:T(8,128)(2,1)} %param.22) | copy-start | bytes 786436
  6.6 116.8 %all-gather.2.cloned.1.call-start = ((), (), s32[]{:S(2)}) async-start(), calls=%async_computation.7 | async-start | bytes 9437184 | tf_op jit(solution)/shard_map/all_gather | solution.py:32
  11.4 0.7 copy-start.5
  11.4 0.9 copy-start.1
  11.4 51.5 %copy-start.6 = (s32[32,1,32]{2,1,0:T(1,128)S(1)}, s32[32,1,32]{2,1,0:T(1,128)}, u32[]{:S(2)}) copy-start(s32[32,1,32]{2,1,0:T(1,128)} %param.17) | copy-start | bytes 12292
  11.4 52.3 %copy-start.9 = (s32[32,1]{0,1:T(1,128)S(1)}, s32[32,1]{0,1:T(1,128)}, u32[]{:S(2)}) copy-start(s32[32,1]{0,1:T(1,128)} %param.18) | copy-start | bytes 388
  11.4 52.9 %copy-start.7 = (f32[32,1,32]{2,1,0:T(1,128)S(1)}, f32[32,1,32]{2,1,0:T(1,128)}, u32[]{:S(2)}) copy-start(f32[32,1,32]{2,1,0:T(1,128)} %param.19) | copy-start | bytes 12292
  16.6 87.7 %all-to-all-start = ((bf16[32,32,128]{2,1,0:T(8,128)(2,1)}), bf16[32,32,128]{2,1,0:T(8,128)(2,1)S(1)}, u32[]{:S(2)}, u32[]{:S(2)}) async-start(bf16[32,32,128]{2,1,0:T(8,128)(2,1)} %bitcast.2), calls=%async_computation | async-start | bytes 524288 | tf_op jit(solution)/shard_map/all_to_all | solution.py:101
  111.6 11.3 %all-to-all-start.1 = ((bf16[4,128,256]{2,1,0:T(8,128)(2,1)}), bf16[4,128,256]{2,1,0:T(8,128)(2,1)S(1)}, u32[]{:S(2)}, u32[]{:S(2)}) async-start(bf16[4,128,256]{2,1,0:T(8,128)(2,1)} %broadcast_in_dim.65), calls=%async_computation.1 | async-start | bytes 524288 | tf_op jit(solution)/shard_map/all_to_all | solution.py:14
  123.3 1.4 slice-start
  125.6 6.9 %collective-permute-start.1 = (bf16[2,64,256]{1,2,0:T(8,128)(2,1)S(1)}, bf16[2,64,256]{1,2,0:T(8,128)(2,1)S(1)}, u32[]{:S(2)}, u32[]{:S(2)}) collective-permute-start(bf16[2,64,256]{1,2,0:T(8,128)(2,1)S(1)} %get-tuple-element.10), channel_id=1, source_target_pairs={{8,0},{16,8},{24,16},{32,24},{40,32},{48,40},{56,48},{64,56},{72,6... | collective-permute-start | bytes 196616 | tf_op jit(solution)/shard_map/ppermute | solution.py:50
  126.9 7.1 %collective-permute-start = (bf16[2,64,256]{1,2,0:T(8,128)(2,1)S(1)}, bf16[2,64,256]{1,2,0:T(8,128)(2,1)S(1)}, u32[]{:S(2)}, u32[]{:S(2)}) collective-permute-start(bf16[2,64,256]{1,2,0:T(8,128)(2,1)S(1)} %get-tuple-element.9), channel_id=1, source_target_pairs={{0,8},{8,16},{16,24},{24,32},{32,40},{40,48},{48,56},{56,64},{64,7... | collective-permute-start | bytes 196616 | tf_op jit(solution)/shard_map/ppermute | solution.py:47
  137.2 15.2 %all-to-all-start.2 = ((bf16[4,128,1024]{2,1,0:T(8,128)(2,1)}), bf16[4,128,1024]{2,1,0:T(8,128)(2,1)S(1)}, u32[]{:S(2)}, u32[]{:S(2)}) async-start(bf16[4,128,1024]{2,1,0:T(8,128)(2,1)} %broadcast_in_dim.68), calls=%async_computation.2 | async-start | bytes 2097152 | tf_op jit(solution)/shard_map/all_to_all | solution.py:14
  156.5 15.7 %copy-start.8 = (bf16[256,128]{1,0:T(8,128)(2,1)S(1)}, bf16[256,128]{1,0:T(8,128)(2,1)}, u32[]{:S(2)}) copy-start(bf16[256,128]{1,0:T(8,128)(2,1)} %param.25) | copy-start | bytes 196612
  157.6 14.4 %all-to-all-start.3 = ((bf16[4,128,1024]{2,1,0:T(8,128)(2,1)}), bf16[4,128,1024]{2,1,0:T(8,128)(2,1)S(1)}, u32[]{:S(2)}, u32[]{:S(2)}) async-start(bf16[4,128,1024]{2,1,0:T(8,128)(2,1)} %broadcast_in_dim.69), calls=%async_computation.3 | async-start | bytes 2097152 | tf_op jit(solution)/shard_map/all_to_all | solution.py:14
  173.0 8.7 %all-to-all-start.4 = ((bf16[4,128,32]{1,2,0:T(8,128)(2,1)}), bf16[4,128,32]{1,2,0:T(8,128)(2,1)S(1)}, u32[]{:S(2)}, u32[]{:S(2)}) async-start(bf16[4,128,32]{1,2,0:T(8,128)(2,1)} %bitcast.27), calls=%async_computation.4 | async-start | bytes 65536 | tf_op jit(solution)/shard_map/all_to_all | solution.py:67
  181.9 46.7 %copy-start.10 = (s32[512]{0:T(512)S(1)}, s32[512]{0:T(512)}, u32[]{:S(2)}) copy-start(s32[512]{0:T(512)} %param.15) | copy-start | bytes 6148
  181.9 52.8 %copy-start.4 = (bf16[512,128]{1,0:T(8,128)(2,1)S(1)}, bf16[512,128]{1,0:T(8,128)(2,1)}, u32[]{:S(2)}) copy-start(bf16[512,128]{1,0:T(8,128)(2,1)} %param.14) | copy-start | bytes 393220
  185.8 32.3 %all-to-all-start.5 = ((bf16[32,2,512]{2,1,0:T(2,128)(2,1)}), bf16[32,2,512]{2,1,0:T(2,128)(2,1)S(1)}, u32[]{:S(2)}, u32[]{:S(2)}) async-start(bf16[32,2,512]{2,1,0:T(2,128)(2,1)} %reshape.330), calls=%async_computation.5 | async-start | bytes 131072 | tf_op jit(solution)/shard_map/all_to_all | solution.py:159
  225.2 9.3 %all-to-all-start.6 = ((bf16[4,512,32]{1,2,0:T(8,128)(2,1)}), bf16[4,512,32]{1,2,0:T(8,128)(2,1)S(1)}, u32[]{:S(2)}, u32[]{:S(2)}) async-start(bf16[4,512,32]{1,2,0:T(8,128)(2,1)} %broadcast_in_dim.71), calls=%async_computation.6 | async-start | bytes 262144 | tf_op jit(solution)/shard_map/all_to_all | solution.py:14
Sparse Core Ops, SparseCore 0:
  11.6 59.8 all-gather.1
where the time goes:
time: 243 us; the launch traced here: 242 us
  waiting for transfers between devices  105 us (43%)
  starting transfers between devices  78.9 us (32%)
  local copies, waits for them, and re-layouts  19.4 us (8%)
  other arithmetic  18 us (7%)
  between operations  13.9 us (6%)
  matrix products  7.24 us (3%)
    all_to_all x1, starting transfers between devices, body(): lax.all_to_all(picked, 'grid', split_axis=0, concat_axis=0, tiled=True)  45.8 us
    all_to_all x1, waiting for transfers between devices, body(): lax.all_to_all(picked, 'grid', split_axis=0, concat_axis=0, tiled=True)  39.1 us
    all_to_all x4, waiting for transfers between devices, copy_for_each(): return lax.all_to_all(copies, axis, split_axis=0, concat_axis=0, tiled=True)  34.3 us
    all_to_all x1, waiting for transfers between devices, body(): lax.all_to_all(outgoing.astype(jnp.bfloat16), 'grid', split_axis=0, conca...  23.6 us
    all_to_all x4, starting transfers between devices, copy_for_each(): return lax.all_to_all(copies, axis, split_axis=0, concat_axis=0, tiled=True)  15.2 us
    all_to_all x1, starting transfers between devices, body(): lax.all_to_all(outgoing.astype(jnp.bfloat16), 'grid', split_axis=0, conca...  8.66 us
    scatter-add x1, other arithmetic, body(): jax.ops.segment_sum(returned.reshape(-1, part_width), sources, num_segmen...  6.13 us
    scatter-add x1, other arithmetic, body(): jax.ops.segment_sum(latent * weights[:, None], targets, num_segments=M_DEV)  6.08 us
  transfers between devices with their start and end apart: 10, of which 9 were waited for; matrix products, arithmetic and copies ran while one was open for 6% of the time, Pallas kernels for 0%

commit v1 on v0

v1 whole, which is shorter than its diff:
```python
import functools
import math

import jax
import jax.numpy as jnp
from jax import lax
from jax.experimental import pallas as pl
from jax.experimental.pallas import tpu as pltpu
from jax.sharding import PartitionSpec as P

HEADS = 16
M_DEV = 128
WINDOW = 64
EMBED, OUT, DEC, STATE, ATT, MLP, PROJ, BACK = STAGES = range(8)
F32 = jnp.float32
BF16 = jnp.bfloat16
MESH = pl.DeviceIdType.MESH


def dot(left, right):
    return jnp.dot(left, right, preferred_element_type=F32)


def dot_tn(left, right):
    return lax.dot_general(left, right, (((0,), (0,)), ((), ())), preferred_element_type=F32)


def dot_nt(left, right):
    return lax.dot_general(left, right, (((1,), (1,)), ((), ())), preferred_element_type=F32)


def exact_dot(left, right):
    return jnp.dot(left, right, precision=lax.Precision.HIGHEST, preferred_element_type=F32)


def gelu(x):
    return 0.5 * x * (1.0 + jnp.tanh(math.sqrt(2.0 / math.pi) * (x + 0.044715 * (x * x * x))))


def rms_norm(values):
    return values * lax.rsqrt(jnp.mean(values * values, axis=-1, keepdims=True) + 1e-06)


def halves(values):
    high = values.astype(BF16)
    return high, (values - high.astype(F32)).astype(BF16)


def near_first(count, stride, ring):
    return sorted(range(count), key=lambda r: min(stride * r + stride // 2, ring - stride * r - stride // 2))


def step_kernel(
    n_grid, n_band, head_dim,
    grid_in, src_in, dst_in, count_in, weight_in, embed_in, qkv_in, out_in, up_in, down_in, dec_in,
    decoded_ref,
    grid_v, src_v, dst_v, count_v, weight_v, embed_v, qkv_v, out_v, up_v, down_v, dec_v,
    pick, select, send_z, states, near_kv, attended, stream_v, product, pieces, proj, back_z, returned,
    load_sem, z_send, z_recv, x_send, x_recv, mem_send, mem_recv,
):
    me = lax.axis_index("grid")
    band = lax.axis_index("band")
    mem = lax.axis_index("mem")
    other = 1 - mem
    per = n_grid // n_band
    slots = src_v.shape[1]
    group = per * slots
    cls = lax.rem(band - me + n_grid, n_band)
    near = lax.rem(band + 2 * (n_grid - me), n_band)
    own_class, own_place = lax.rem(me, n_band), me // n_band
    is_self = near == 0
    up_next, down_next = lax.rem(me + 1, n_grid), lax.rem(me + n_grid - 1, n_grid)
    bands = [lax.rem(band + q, n_band) for q in range(n_band)]
    far_bands = sorted(range(1, n_band), key=lambda q: -min(q, n_band - q))
    near_bands = far_bands[::-1]
    order = near_first(per, n_band, n_grid)

    def z_peer(r):
        return lax.rem(me + near + n_band * r, n_grid)

    barrier = pltpu.get_barrier_semaphore()

    def greet(device):
        pl.semaphore_signal(barrier, inc=1, device_id=device, device_id_type=MESH)

    for r in order[::-1]:
        if r == 0:
            @pl.when(jnp.logical_not(is_self))
            def _():
                greet({"grid": z_peer(0)})
        else:
            greet({"grid": z_peer(r)})
    greet({"grid": up_next})
    greet({"grid": down_next})
    for q in far_bands:
        greet({"band": bands[q]})
    greet({"mem": other})

    loads = [
        pltpu.make_async_copy(source, target, load_sem.at[k])
        for k, (source, target) in enumerate(
            (
                (src_in, src_v), (dst_in, dst_v), (count_in, count_v), (weight_in, weight_v), (grid_in, grid_v),
                (embed_in, embed_v.at[band]), (qkv_in, qkv_v.at[mem]), (out_in, out_v.at[band, mem]),
                (up_in, up_v.at[mem]), (down_in, down_v.at[mem]), (dec_in, dec_v.at[band]),
            )
        )
    ]
    for load in loads:
        load.start()
    for load in loads[:5]:
        load.wait()

    slot_of = lax.broadcasted_iota(jnp.int32, (slots, group), 1)
    spread = jnp.where(lax.rem(slot_of, slots) == lax.broadcasted_iota(jnp.int32, (slots, group), 0), 1.0, 0.0).astype(F32)
    shard_row = lax.broadcasted_iota(jnp.int32, (n_grid, group), 0)
    place_lane = lax.broadcasted_iota(jnp.int32, (n_grid, group), 1) // slots
    square_row = lax.broadcasted_iota(jnp.int32, (n_grid, n_grid), 0)
    square_lane = lax.broadcasted_iota(jnp.int32, (n_grid, n_grid), 1)
    counts = jnp.sum(
        jnp.where(square_row == square_lane, count_v[...].astype(F32), 0.0), axis=1, keepdims=True
    )
    slot_lane = lax.broadcasted_iota(jnp.int32, (n_grid, slots), 1).astype(F32)
    live = jnp.where(slot_lane < counts, weight_v[:, 0, :], 0.0)
    src_wide = exact_dot(src_v[...].astype(F32), spread)
    dst_wide = exact_dot(dst_v[:, 0, :].astype(F32), spread)
    live_wide = exact_dot(live, spread)

    def lane_row(wide, c):
        return jnp.sum(jnp.where(shard_row == c + n_band * place_lane, wide, 0.0), axis=0, keepdims=True)

    def build_pick(c):
        point = lax.broadcasted_iota(jnp.int32, (grid_v.shape[0], group), 0).astype(F32)
        pick[c] = jnp.where(point == lane_row(src_wide, c), 1.0, 0.0).astype(BF16)

    def build_select(c):
        rows = stream_v.shape[0]
        node = lax.broadcasted_iota(jnp.int32, (rows, group), 0).astype(F32)
        table = jnp.where(node == lane_row(dst_wide, c), lane_row(live_wide, c), 0.0)
        high, low = halves(table)
        select[c, 0:rows] = high
        select[c, rows : 2 * rows] = low

    build_pick(cls)
    send_z[...] = dot_tn(pick[cls], grid_v[...]).astype(BF16).reshape(send_z.shape)
    for c in range(n_band):
        build_select(c)
    for load in loads[5:]:
        load.wait()

    pl.semaphore_wait(barrier, per + 2 + n_band - jnp.where(is_self, 1, 0))

    def z_copy(way, r, source, target):
        peer = z_peer(r)
        return pltpu.make_async_remote_copy(
            src_ref=source.at[peer // n_band], dst_ref=target.at[own_class, own_place],
            send_sem=z_send.at[way, r], recv_sem=z_recv.at[way, own_place],
            device_id={"grid": peer}, device_id_type=MESH,
        )

    def z_arrival(way, r, source, target):
        peer = z_peer(r)
        return pltpu.make_async_remote_copy(
            src_ref=source.at[peer // n_band], dst_ref=target.at[cls, peer // n_band],
            send_sem=z_send.at[way, r], recv_sem=z_recv.at[way, peer // n_band],
            device_id={"grid": peer}, device_id_type=MESH,
        )

    def z_own(way, source, target):
        return pltpu.make_async_copy(source.at[own_place], target.at[cls, own_place], z_recv.at[way, own_place])

    def z_start(way, source, target):
        for r in order[::-1]:
            if r == 0:
                @pl.when(is_self)
                def _():
                    z_own(way, source, target).start()

                @pl.when(jnp.logical_not(is_self))
                def _():
                    z_copy(way, 0, source, target).start()
            else:
                z_copy(way, r, source, target).start()

    def z_wait(way, r, source, target):
        if r == 0:
            @pl.when(is_self)
            def _():
                z_own(way, source, target).wait()

            @pl.when(jnp.logical_not(is_self))
            def _():
                z_arrival(way, 0, source, target).wait_recv()
        else:
            z_arrival(way, r, source, target).wait_recv()

    def z_sent(way, source, target):
        for r in order:
            if r == 0:
                @pl.when(jnp.logical_not(is_self))
                def _():
                    z_copy(way, 0, source, target).wait_send()
            else:
                z_copy(way, r, source, target).wait_send()

    def x_copy(stage, q, source, target):
        return pltpu.make_async_remote_copy(
            src_ref=source, dst_ref=target, send_sem=x_send.at[stage, q], recv_sem=x_recv.at[stage, n_band - q],
            device_id={"band": bands[q]}, device_id_type=MESH,
        )

    def x_wait(stage, q, target):
        pltpu.make_async_remote_copy(
            src_ref=target, dst_ref=target, send_sem=x_send.at[stage, q], recv_sem=x_recv.at[stage, q],
            device_id={"band": bands[q]}, device_id_type=MESH,
        ).wait_recv()

    def mem_copy(k, source, target):
        return pltpu.make_async_remote_copy(
            src_ref=source, dst_ref=target, send_sem=mem_send.at[k], recv_sem=mem_recv.at[k],
            device_id={"mem": other}, device_id_type=MESH,
        )


    def gather_start(stage, ref, index):
        copies = [x_copy(stage, q, ref.at[index], ref.at[index]) for q in far_bands]
        for copy in copies:
            copy.start()
        return copies

    z_start(0, send_z, states)
    sent = gather_start(EMBED, embed_v, band)
    shared = [
        mem_copy(0, qkv_v.at[mem], qkv_v.at[mem]),
        mem_copy(1, up_v.at[mem], up_v.at[mem]),
        mem_copy(2, down_v.at[mem], down_v.at[mem]),
        mem_copy(3, out_v.at[band, mem], out_v.at[band, mem]),
    ]
    for copy in shared:
        copy.start()
    out_sent = [x_copy(OUT, q, out_v.at[band, mem], out_v.at[band, mem]) for q in far_bands]
    for copy in out_sent:
        copy.start()
    sent += out_sent

    for c in range(n_band):
        @pl.when(c != cls)
        def _():
            build_pick(c)

    def pass_on(r, ref, stage):
        place = z_peer(r) // n_band
        for q in far_bands:
            x_copy(stage, q, ref.at[cls, place], ref.at[cls, place]).start()

    for r in order:
        z_wait(0, r, send_z, states)
        pass_on(r, states, STATE)
    sent += gather_start(DEC, dec_v, band)

    rows = stream_v.shape[0]
    width = embed_v.shape[2]
    for q in near_bands:
        x_wait(EMBED, q, embed_v.at[bands[q]])
    for q in [0] + near_bands:
        c = lax.rem(cls + q, n_band)
        if q:
            x_wait(STATE, q, states.at[c])
        block = states[c].reshape(group, -1)
        for col in range(n_band):
            latent = gelu(dot(block, embed_v[col])).astype(BF16)
            both = dot(select[c], latent)
            part = both[:rows] + both[rows:]
            cols = slice(col * width, (col + 1) * width)
            stream_v[:, cols] = part if q == 0 else stream_v[:, cols] + part
    stream = stream_v[...].astype(BF16).astype(F32)
    normed = rms_norm(stream).astype(BF16)

    mem_copy(0, qkv_v.at[other], qkv_v.at[other]).wait_recv()
    deep = qkv_v.shape[2]

    def project(which):
        return dot(normed[:, :deep], qkv_v[0, which]) + dot(normed[:, deep:], qkv_v[1, which])

    lane_r = lax.broadcasted_iota(jnp.int32, (width, width), 0) // head_dim
    lane_c = lax.broadcasted_iota(jnp.int32, (width, width), 1) // head_dim
    head_mean = jnp.where(lane_r == lane_c, 1.0 / head_dim, 0.0).astype(BF16)

    def head_norm(values):
        high, low = halves(values * values)
        return values * lax.rsqrt(dot(high, head_mean) + dot(low, head_mean) + 1e-06)

    near_kv[0:rows, 0:width] = head_norm(project(1)).astype(BF16)
    near_kv[0:rows, width:] = project(2).astype(BF16)
    lower, upper = pl.ds(rows, WINDOW), pl.ds(rows + WINDOW, WINDOW)

    def halo(k, source, target, device):
        return pltpu.make_async_remote_copy(
            src_ref=near_kv.at[source], dst_ref=near_kv.at[target], send_sem=mem_send.at[k], recv_sem=mem_recv.at[k],
            device_id={"grid": device}, device_id_type=MESH,
        )

    n_shared = 4 + n_band - 1
    to_next = halo(n_shared, pl.ds(rows - WINDOW, WINDOW), lower, up_next)
    to_last = halo(n_shared + 1, pl.ds(0, WINDOW), upper, down_next)
    to_next.start()
    to_last.start()

    for q in near_bands:
        x_wait(OUT, q, out_v.at[bands[q], mem])
        copy = mem_copy(3 + q, out_v.at[bands[q], mem], out_v.at[bands[q], mem])
        copy.start()
        shared.append(copy)

    n_heads = width // head_dim
    query = head_norm(project(0)).astype(BF16) * jnp.asarray(head_dim**-0.5, BF16)
    head_lane = lax.broadcasted_iota(jnp.int32, (rows, width), 1) // head_dim
    zero = jnp.zeros_like(query)
    heads = jnp.concatenate([jnp.where(head_lane == h, query, zero) for h in range(n_heads)], axis=0)
    tall = n_heads * rows
    q_pos = lax.rem(lax.broadcasted_iota(jnp.int32, (tall, rows), 0), rows)
    k_pos = lax.broadcasted_iota(jnp.int32, (tall, rows), 1)
    own_scores = dot_nt(heads, near_kv[0:rows, 0:width])
    own_exp = jnp.where(jnp.abs(q_pos - k_pos) <= WINDOW, jnp.exp(own_scores), 0.0)
    to_next.wait()
    to_last.wait()
    far_pos = jnp.where(k_pos < WINDOW, k_pos - WINDOW, k_pos + rows - WINDOW)
    first, last = me == 0, me == n_grid - 1
    low_pos = jnp.where(first, 0, -WINDOW)
    high_pos = jnp.where(last, rows, rows + WINDOW)
    far_ok = (jnp.abs(q_pos - far_pos) <= WINDOW) & (far_pos >= low_pos) & (far_pos < high_pos)
    far_exp = jnp.where(far_ok, jnp.exp(dot_nt(heads, near_kv[rows:, 0:width])), 0.0)
    total = jnp.sum(own_exp, axis=-1, keepdims=True) + jnp.sum(far_exp, axis=-1, keepdims=True)
    mixed = dot((own_exp / total).astype(BF16), near_kv[0:rows, width:])
    mixed += dot((far_exp / total).astype(BF16), near_kv[rows:, width:])
    joined = mixed[0:rows]
    for h in range(1, n_heads):
        joined = jnp.where(head_lane == h, mixed[h * rows : (h + 1) * rows], joined)
    attended[band] = joined.astype(BF16)
    sent += gather_start(ATT, attended, band)

    half = out_v.shape[3]
    mem_copy(3, out_v.at[band, other], out_v.at[band, other]).wait_recv()
    sums = [0.0, 0.0]
    for q in [0] + near_bands:
        if q:
            x_wait(ATT, q, attended.at[bands[q]])
            mem_copy(3 + q, out_v.at[bands[q], other], out_v.at[bands[q], other]).wait_recv()
        left = attended[bands[q]]
        for m in range(2):
            sums[m] = sums[m] + dot(left, out_v[bands[q], m]).astype(BF16).astype(F32)
    stream = stream + jnp.concatenate(sums, axis=1)
    stream_v[...] = stream
    normed = rms_norm(stream).astype(BF16)

    mem_copy(1, up_v.at[other], up_v.at[other]).wait_recv()
    mem_copy(2, down_v.at[other], down_v.at[other]).wait_recv()
    deep = up_v.shape[1]
    hidden = gelu(dot(normed[:, :deep], up_v[0]) + dot(normed[:, deep:], up_v[1])).astype(BF16)
    for m in range(2):
        product[:, m * half : (m + 1) * half] = dot(hidden, down_v[m]).astype(BF16)

    share = rows // n_band
    for q in far_bands:
        copy = x_copy(MLP, q, product.at[pl.ds(pl.multiple_of(bands[q] * share, share), share)], pieces.at[q])
        copy.start()
        sent.append(copy)
    own_rows = pl.ds(pl.multiple_of(band * share, share), share)
    stream = stream_v[own_rows] + product[own_rows].astype(F32)
    for q in near_bands:
        x_wait(DEC, q, dec_v.at[bands[q]])
    for q in near_bands:
        x_wait(MLP, q, pieces.at[n_band - q])
        stream = stream + pieces[n_band - q].astype(F32)
    mesh_out = stream.astype(BF16)
    decoded = dot(mesh_out[:, :width], dec_v[0])
    for k in range(1, n_band):
        decoded += dot(mesh_out[:, k * width : (k + 1) * width], dec_v[k])
    proj[band] = decoded.astype(BF16)
    sent += gather_start(PROJ, proj, band)
    for q in near_bands:
        x_wait(PROJ, q, proj.at[bands[q]])

    nodes = proj[...].reshape(rows, -1)
    z_sent(0, send_z, states)
    outgoing = dot_tn(select[cls, 0:rows], nodes) + dot_tn(select[cls, rows : 2 * rows], nodes)
    back_z[...] = outgoing.astype(BF16).reshape(back_z.shape)
    z_start(1, back_z, returned)

    for q in far_bands:
        x_copy(STATE, q, states.at[cls], states.at[cls]).wait_send()
    for copy in sent + shared:
        copy.wait_send()

    for r in order:
        z_wait(1, r, back_z, returned)
        pass_on(r, returned, BACK)
    decoded_ref[...] = dot(pick[cls], returned[cls].reshape(group, -1))
    for q in near_bands:
        c = lax.rem(cls + q, n_band)
        x_wait(BACK, q, returned.at[c])
        decoded_ref[...] += dot(pick[c], returned[c].reshape(group, -1))
    z_sent(1, back_z, returned)
    for q in far_bands:
        x_copy(BACK, q, returned.at[cls], returned.at[cls]).wait_send()


def body(
    grid_state, forcing, boundary_mask, edge_src, edge_dst, edge_count, edge_weight,
    embed_weight, attn_qkv, attn_out, mlp_in, mlp_out, decode_weight,
):
    n_grid, n_band, n_mem = lax.axis_size("grid"), lax.axis_size("band"), lax.axis_size("mem")
    grid_rows = grid_state[0]
    points, channels = grid_rows.shape
    slots = edge_src.shape[2]
    model = decode_weight.shape[0] * n_band
    width = embed_weight.shape[1]
    rows = M_DEV
    per = n_grid // n_band
    group = per * slots
    operands = (
        grid_rows, edge_src[0], edge_dst, edge_count.T, edge_weight, embed_weight,
        jnp.swapaxes(attn_qkv[0], 0, 1), attn_out[0], mlp_in[0], mlp_out[0], decode_weight,
    )
    vmem = pltpu.VMEM
    scratch = [
        vmem(operands[0].shape, BF16),
        vmem(operands[1].shape, jnp.int32),
        vmem(operands[2].shape, jnp.int32),
        vmem(operands[3].shape, jnp.int32),
        vmem(operands[4].shape, F32),
        vmem((n_band, *operands[5].shape), BF16),
        vmem((n_mem, *operands[6].shape), BF16),
        vmem((n_band, n_mem, *operands[7].shape), BF16),
        vmem((n_mem, *operands[8].shape), BF16),
        vmem((n_mem, *operands[9].shape), BF16),
        vmem((n_band, *operands[10].shape), BF16),
        vmem((n_band, points, group), BF16),
        vmem((n_band, 2 * rows, group), BF16),
        vmem((per, slots, channels), BF16),
        vmem((n_band, per, slots, channels), BF16),
        vmem((rows + 2 * WINDOW, 2 * width), BF16),
        vmem((n_band, rows, width), BF16),
        vmem((rows, model), F32),
        vmem((rows, model), BF16),
        vmem((n_band, rows // n_band, model), BF16),
        vmem((n_band, rows // n_band, channels), BF16),
        vmem((per, slots, channels), BF16),
        vmem((n_band, per, slots, channels), BF16),
        pltpu.SemaphoreType.DMA((11,)),
        pltpu.SemaphoreType.DMA((2, per)),
        pltpu.SemaphoreType.DMA((2, per)),
        pltpu.SemaphoreType.DMA((len(STAGES), n_band)),
        pltpu.SemaphoreType.DMA((len(STAGES), n_band)),
        pltpu.SemaphoreType.DMA((n_band + 5,)),
        pltpu.SemaphoreType.DMA((n_band + 5,)),
    ]
    decoded = pl.pallas_call(
        functools.partial(step_kernel, n_grid, n_band, model // HEADS),
        out_shape=jax.ShapeDtypeStruct((points, channels), F32),
        in_specs=[pl.BlockSpec(memory_space=pl.ANY)] * len(operands),
        out_specs=pl.BlockSpec(memory_space=pltpu.VMEM),
        scratch_shapes=scratch,
        compiler_params=pltpu.CompilerParams(collective_id=0, has_side_effects=True),
    )(*operands)
    forced = boundary_mask[:, None] == 1
    result = jnp.where(forced, forcing.astype(F32), grid_rows.astype(F32) + decoded)
    return result.astype(BF16)[None]


def solution(mesh):
    return jax.shard_map(
        body,
        mesh=mesh,
        in_specs=(
            P(("dom", "mem"), "grid", None),
            P(("dom", "grid"), None),
            P("grid"),
            P("grid", None, None),
            P(None, "grid", None),
            P(None, "grid"),
            P(None, "grid", None),
            P(None, "band"),
            P(None, "mem", None, "band"),
            P(None, "band", "mem"),
            P(None, "mem", "band"),
            P(None, "band", "mem"),
            P("band", None),
        ),
        out_specs=P(("dom", "mem"), "grid", None),
        check_vma=False,
    )
```

time: 243 us -> 114 us (0.47)
  Pallas kernels: 0 us -> 112 us
  waiting for transfers between devices: 105 us -> 0 us
  starting transfers between devices: 78.9 us -> 0 us
  local copies, waits for them, and re-layouts: 19.4 us -> 0.69 us
  other arithmetic: 18 us -> 1.75 us
  between operations: 13.9 us -> 0.03 us
  matrix products: 7.24 us -> 0 us
    pallas_call x0 -> x1, Pallas kernels: none -> 112 us  [body(): pl.pallas_call(functools.partial(step_kernel, n_grid, n_band, model // HE...]
    all_to_all x7 -> x0, waiting for transfers between devices: 102 us -> none  [the longest x1 39.1 us: body(): lax.all_to_all(picked, 'grid', split_axis=0, concat_axis=0, tiled=True)]
    all_to_all x7 -> x0, starting transfers between devices: 73 us -> none  [the longest x1 45.8 us: body(): lax.all_to_all(picked, 'grid', split_axis=0, concat_axis=0, tiled=True)]
    scatter-add x2 -> x0, other arithmetic: 12.2 us -> none  [the longest x1 6.13 us: body(): jax.ops.segment_sum(returned.reshape(-1, part_width), sources, num_segmen...]
    dot_general x7 -> x0, matrix products: 7.24 us -> none  [the longest x1 3.46 us: body(): jnp.dot(hidden, w_back, preferred_element_type=jnp.float32)]
    gather x2 -> x0, local copies, waits for them, and re-layouts: 7.1 us -> none  [the longest x1 4.29 us: body(): picked = grid_rows[sources].reshape(shards, slot_count, var_count)]
    ppermute x2 -> x0, starting transfers between devices: 5.91 us -> none  [the longest x1 4.6 us: extended(): lax.ppermute(lax.slice_in_dim(block, block.shape[dim] - width, None, axis...]
    unnamed x28 -> x6, local copies, waits for them, and re-layouts: 5.86 us -> 0.69 us
  transfers between devices with their start and end apart: 10 -> 0, of which waited for: 9 -> 0; matrix products, arithmetic and copies ran while one was open for 6% -> 0% of each run, Pallas kernels for 0% -> 0%
where the time goes in v1:
time: 114 us
  Pallas kernels  112 us (98%)
  other arithmetic  1.75 us (2%)
    pallas_call x1, Pallas kernels, body(): pl.pallas_call(functools.partial(step_kernel, n_grid, n_band, model // HE...  112 us

profile of v1, /device:TPU:40, one launch (start us, length us, event | category | flops | bytes accessed | tf_op | source)
XLA Modules:
  0.0 114.0 jit_solution(17925246279738595877)
XLA Ops:
  0.0 0.0 copy-start.2
  0.0 0.7 copy-done.2
  0.7 0.0 copy-start
  0.7 0.0 copy-start.1
  0.7 111.5 %shard_map.127 = f32[512,128]{1,0:T(8,128)} custom-call(bf16[512,128]{1,0:T(8,128)(2,1)} %bitcast.15, s32[32,32]{1,0:T(8,128)} %bitcast.17, s32[32,1,32]{2,1,0:T(1,128)} %dst_in.1, s32[1,32]{1,0:T(1,128)} %bitcast.18, f32[32,1,32]{2,1,0:T(1,128)} %weight_in.1, bf16[128,256]{1,0:T(8,128)(2,1)} %embed_in.1, bf16[3,512,256]{2,1,0:T(8,128)(2,1)} %bitcast.14, ...), custom_call_target="tpu_custom_call" | custom-call | tf_op jit(solution)/shard_map/pallas_call | solution.py:458
  112.2 0.0 copy-done
  112.2 0.0 copy-done.1
  112.3 1.7 %fusion = bf16[1,512,128]{2,1,0:T(8,128)(2,1)} fusion(f32[512,128]{1,0:T(8,128)} %shard_map.127, bf16[512,128]{1,0:T(8,128)(2,1)S(1)} %copy-done.1, pred[512]{0:T(512)(128)(4,1)S(1)} %broadcast_compare_fusion, bf16[1,512,128]{2,1,0:T(8,128)(2,1)S(1)} %copy-done), kind=kLoop, calls=%fused_computation.1 | loop fusion | flops 327680 | bytes 655872 | tf_op jit(solution)/shard_map/broadcast_in_dim | solution.py:468
  (1 shorter events, 0.0 us)
Async XLA Ops:
  0.0 0.7 copy-start.2
  0.7 111.6 %copy-start = (bf16[1,512,128]{2,1,0:T(8,128)(2,1)S(1)}, bf16[1,512,128]{2,1,0:T(8,128)(2,1)}, u32[]{:S(2)}) copy-start(bf16[1,512,128]{2,1,0:T(8,128)(2,1)} %param.13) | copy-start | bytes 393220
  0.7 111.6 %copy-start.1 = (bf16[512,128]{1,0:T(8,128)(2,1)S(1)}, bf16[512,128]{1,0:T(8,128)(2,1)}, u32[]{:S(2)}) copy-start(bf16[512,128]{1,0:T(8,128)(2,1)} %param.14) | copy-start | bytes 393220

commit v2 on v1

v2 whole, which is shorter than its diff:
```python
import functools
import math

import jax
import jax.numpy as jnp
from jax import lax
from jax.experimental import pallas as pl
from jax.experimental.pallas import tpu as pltpu
from jax.sharding import PartitionSpec as P

HEADS = 16
M_DEV = 128
WINDOW = 64
EMBED, OUT, PASS, DEC, ATT, PROJ, *MORE = STAGES = range(10)
STATES, BACKS = MORE[:2], MORE[2:]
F32 = jnp.float32
BF16 = jnp.bfloat16
MESH = pl.DeviceIdType.MESH


def dot(left, right):
    return jnp.dot(left, right, preferred_element_type=F32)


def dot_tn(left, right):
    return lax.dot_general(left, right, (((0,), (0,)), ((), ())), preferred_element_type=F32)


def dot_nt(left, right):
    return lax.dot_general(left, right, (((1,), (1,)), ((), ())), preferred_element_type=F32)


def exact_dot(left, right):
    return jnp.dot(left, right, precision=lax.Precision.HIGHEST, preferred_element_type=F32)


def gelu(x):
    return 0.5 * x * (1.0 + jnp.tanh(math.sqrt(2.0 / math.pi) * (x + 0.044715 * (x * x * x))))


def rms_norm(values):
    return values * lax.rsqrt(jnp.mean(values * values, axis=-1, keepdims=True) + 1e-06)


def halves(values):
    high = values.astype(BF16)
    return high, (values - high.astype(F32)).astype(BF16)


def near_first(count, stride, ring):
    return sorted(range(count), key=lambda r: min(stride * r + stride // 2, ring - stride * r - stride // 2))


def step_kernel(
    n_grid, n_band, head_dim,
    grid_in, forcing_in, mask_in, src_in, dst_in, count_in, weight_in, embed_in, qkv_in, out_in, up_in, down_in, dec_in,
    next_ref,
    grid_v, forcing_v, mask_v, src_v, dst_v, count_v, weight_v, embed_v, qkv_v, out_v, up_v, down_v, dec_v,
    pick, select, free_v, send_z, states, near_kv, attended, stream_v, fold_v, proj, back_z, returned,
    load_sem, z_send, z_recv, x_send, x_recv, mem_send, mem_recv,
):
    me = lax.axis_index("grid")
    band = lax.axis_index("band")
    mem = lax.axis_index("mem")
    other = 1 - mem
    per = n_grid // n_band
    slots = src_v.shape[1]
    group = per * slots
    up_next, down_next = lax.rem(me + 1, n_grid), lax.rem(me + n_grid - 1, n_grid)
    bands = [lax.rem(band + q, n_band) for q in range(n_band)]
    far_bands = sorted(range(1, n_band), key=lambda q: -min(q, n_band - q))
    near_bands = far_bands[::-1]
    beside, across = (1, n_band - 1), n_band // 2
    order = near_first(per, n_band, n_grid)
    place_of = {r: p for p, r in enumerate(order)}
    near = [lax.rem(bands[q] + 2 * (n_grid - me), n_band) for q in range(n_band)]
    is_self = near[0] == 0

    def z_peer(p):
        return lax.rem(me + near[0] + n_band * order[p], n_grid)

    def place_there(p):
        r = order[p]
        return jnp.where(is_self, place_of[(per - r) % per], place_of[per - 1 - r])

    barrier = pltpu.get_barrier_semaphore()

    def greet(device):
        pl.semaphore_signal(barrier, inc=1, device_id=device, device_id_type=MESH)

    for p in range(per)[::-1]:
        if order[p] == 0:
            @pl.when(jnp.logical_not(is_self))
            def _():
                greet({"grid": z_peer(p)})
        else:
            greet({"grid": z_peer(p)})
    greet({"grid": up_next})
    greet({"grid": down_next})
    for q in far_bands:
        greet({"band": bands[q]})
    greet({"mem": other})

    half = dec_v.shape[2]
    loads = [
        pltpu.make_async_copy(source, target, load_sem.at[k])
        for k, (source, target) in enumerate(
            (
                (src_in, src_v), (grid_in, grid_v), (embed_in, embed_v.at[band]),
                (dst_in, dst_v), (count_in, count_v), (weight_in, weight_v), (mask_in, mask_v), (forcing_in, forcing_v),
                (qkv_in, qkv_v.at[mem]), (out_in, out_v.at[band, mem]), (up_in, up_v.at[mem]), (down_in, down_v.at[mem]),
                (dec_in.at[0:half], dec_v.at[band, 0]), (dec_in.at[half : 2 * half], dec_v.at[band, 1]),
            )
        )
    ]
    for load in loads:
        load.start()

    lane = lax.broadcasted_iota(jnp.int32, (slots, group), 1)
    spread = jnp.where(lax.rem(lane, slots) == lax.broadcasted_iota(jnp.int32, (slots, group), 0), 1.0, 0.0).astype(F32)
    shard_row = lax.broadcasted_iota(jnp.int32, (n_grid, group), 0)
    place_lane = lax.broadcasted_iota(jnp.int32, (n_grid, group), 1) // slots
    step_lane = jnp.zeros_like(place_lane)
    for p in range(per):
        step_lane = jnp.where(place_lane == p, n_band * order[p], step_lane)

    def lane_row(wide, q):
        mine = shard_row == lax.rem(step_lane + (me + near[q]), n_grid)
        return jnp.sum(jnp.where(mine, wide, 0.0), axis=0, keepdims=True)

    def build_pick(q):
        point = lax.broadcasted_iota(jnp.int32, (grid_v.shape[0], group), 0).astype(F32)
        pick[q] = jnp.where(point == lane_row(src_wide, q), 1.0, 0.0).astype(BF16)

    with jax.named_scope("w_load"):
        loads[0].wait()
        loads[1].wait()
    src_wide = exact_dot(src_v[...].astype(F32), spread)
    build_pick(0)
    send_z[...] = dot_tn(pick[0], grid_v[...]).astype(BF16).reshape(send_z.shape)

    with jax.named_scope("w_barrier"):
        pl.semaphore_wait(barrier, per + 2 + n_band - jnp.where(is_self, 1, 0))

    def z_copy(way, p, source, target):
        there = place_there(p)
        return pltpu.make_async_remote_copy(
            src_ref=source.at[p], dst_ref=target.at[0, there], send_sem=z_send.at[way, p], recv_sem=z_recv.at[way, there],
            device_id={"grid": z_peer(p)}, device_id_type=MESH,
        )

    def z_arrival(way, p, source, target):
        return pltpu.make_async_remote_copy(
            src_ref=source.at[p], dst_ref=target.at[0, p], send_sem=z_send.at[way, p], recv_sem=z_recv.at[way, p],
            device_id={"grid": z_peer(p)}, device_id_type=MESH,
        )

    def z_own(way, p, source, target):
        return pltpu.make_async_copy(source.at[p], target.at[0, p], z_recv.at[way, p])

    def z_start(way, source, target):
        for p in range(per)[::-1]:
            if order[p] == 0:
                @pl.when(is_self)
                def _():
                    z_own(way, p, source, target).start()

                @pl.when(jnp.logical_not(is_self))
                def _():
                    z_copy(way, p, source, target).start()
            else:
                z_copy(way, p, source, target).start()

    def z_wait(way, p, source, target):
        if order[p] == 0:
            @pl.when(is_self)
            def _():
                z_own(way, p, source, target).wait()

            @pl.when(jnp.logical_not(is_self))
            def _():
                z_arrival(way, p, source, target).wait_recv()
        else:
            z_arrival(way, p, source, target).wait_recv()

    def z_sent(way, source, target):
        for p in range(per):
            if order[p] == 0:
                @pl.when(jnp.logical_not(is_self))
                def _():
                    z_copy(way, p, source, target).wait_send()
            else:
                z_copy(way, p, source, target).wait_send()

    def x_copy(stage, q, source, target):
        return pltpu.make_async_remote_copy(
            src_ref=source, dst_ref=target, send_sem=x_send.at[stage, q], recv_sem=x_recv.at[stage, n_band - q],
            device_id={"band": bands[q]}, device_id_type=MESH,
        )

    def x_wait(stage, q, target):
        pltpu.make_async_remote_copy(
            src_ref=target, dst_ref=target, send_sem=x_send.at[stage, q], recv_sem=x_recv.at[stage, q],
            device_id={"band": bands[q]}, device_id_type=MESH,
        ).wait_recv()

    def mem_copy(k, ref):
        return pltpu.make_async_remote_copy(
            src_ref=ref, dst_ref=ref, send_sem=mem_send.at[k], recv_sem=mem_recv.at[k],
            device_id={"mem": other}, device_id_type=MESH,
        )

    sent = []

    def start(copy):
        copy.start()
        sent.append(copy)

    def gather_start(stage, ref):
        for q in far_bands:
            start(x_copy(stage, q, ref, ref))

    QKV, UP, DOWN, OUT_OWN, DEC_OWN, LOW, HIGH = 0, 1, 2, 3, 3 + n_band, 3 + 2 * n_band, 4 + 2 * n_band

    z_start(0, send_z, states)
    with jax.named_scope("w_load2"):
        loads[2].wait()
    gather_start(EMBED, embed_v.at[band])
    with jax.named_scope("w_load3"):
        for load in loads[3:]:
            load.wait()
    for k, ref in ((QKV, qkv_v), (UP, up_v), (DOWN, down_v)):
        start(mem_copy(k, ref.at[mem]))
    start(mem_copy(OUT_OWN, out_v.at[band, mem]))

    rows = stream_v.shape[0]
    square_row = lax.broadcasted_iota(jnp.int32, (n_grid, n_grid), 0)
    square_lane = lax.broadcasted_iota(jnp.int32, (n_grid, n_grid), 1)
    counts = jnp.sum(jnp.where(square_row == square_lane, count_v[...].astype(F32), 0.0), axis=1, keepdims=True)
    slot_lane = lax.broadcasted_iota(jnp.int32, (n_grid, slots), 1).astype(F32)
    live = jnp.where(slot_lane < counts, weight_v[:, 0, :], 0.0)
    dst_wide = exact_dot(dst_v[:, 0, :].astype(F32), spread)
    live_wide = exact_dot(live, spread)
    node = lax.broadcasted_iota(jnp.int32, (rows, group), 0).astype(F32)
    for q in range(n_band):
        table = jnp.where(node == lane_row(dst_wide, q), lane_row(live_wide, q), 0.0)
        high, low = halves(table)
        select[q, 0:rows] = high
        select[q, rows : 2 * rows] = low
    for q in range(1, n_band):
        build_pick(q)
    lanes = mask_v.shape[1]
    diagonal = lax.broadcasted_iota(jnp.int32, (lanes, lanes), 0) == lax.broadcasted_iota(jnp.int32, (lanes, lanes), 1)
    for k in range(mask_v.shape[0]):
        flags = jnp.where(mask_v[k : k + 1, :] == 1, 0.0, 1.0).astype(F32)
        column = jnp.sum(jnp.where(diagonal, flags, 0.0), axis=1, keepdims=True)
        free_v[k * lanes : (k + 1) * lanes] = jnp.broadcast_to(column, (lanes, free_v.shape[1]))

    near_part = per // 2
    parts = (slice(0, near_part), slice(near_part, per))

    def pass_on(p, ref, stages):
        for q in far_bands:
            x_copy(stages[p // near_part], q, ref.at[0, p], ref.at[n_band - q, p]).start()

    def passed_on(ref, stages):
        for k, part in enumerate(parts):
            for q in far_bands:
                x_copy(stages[k], q, ref.at[0, part], ref.at[n_band - q, part]).wait_send()

    width = embed_v.shape[2]

    def encode(k, q, first):
        span = near_part * slots
        block = states[q, parts[k]].reshape(span, -1)
        table = select[q, :, k * span : (k + 1) * span]
        for col in range(n_band):
            both = dot(table, gelu(dot(block, embed_v[col])).astype(BF16))
            part = both[:rows] + both[rows:]
            cols = slice(col * width, (col + 1) * width)
            stream_v[:, cols] = part if first else stream_v[:, cols] + part

    with jax.named_scope("w_znear"):
        for p in range(near_part):
            z_wait(0, p, send_z, states)
            pass_on(p, states, STATES)
    with jax.named_scope("w_embed"):
        for q in near_bands:
            x_wait(EMBED, q, embed_v.at[bands[q]])
    encode(0, 0, True)
    with jax.named_scope("w_zfar"):
        for p in range(near_part, per):
            z_wait(0, p, send_z, states)
            pass_on(p, states, STATES)
    for q in far_bands:
        start(x_copy(DEC, q, dec_v.at[band, mem], dec_v.at[band, mem]))
    for q in beside:
        start(x_copy(OUT, q, out_v.at[band, mem], out_v.at[band, mem]))
    encode(1, 0, False)
    for k in range(2):
        for q in near_bands:
            with jax.named_scope(f"w_x{k}{q}"):
                x_wait(STATES[k], q, states.at[q, parts[k]])
            encode(k, q, False)
    stream = stream_v[...].astype(BF16).astype(F32)
    stream_v[...] = stream
    normed = rms_norm(stream).astype(BF16)

    with jax.named_scope("w_qkv"):
        mem_copy(QKV, qkv_v.at[other]).wait_recv()
    deep = qkv_v.shape[2]

    def project(which):
        return dot(normed[:, :deep], qkv_v[0, which]) + dot(normed[:, deep:], qkv_v[1, which])

    lane_r = lax.broadcasted_iota(jnp.int32, (width, width), 0) // head_dim
    lane_c = lax.broadcasted_iota(jnp.int32, (width, width), 1) // head_dim
    head_mean = jnp.where(lane_r == lane_c, 1.0 / head_dim, 0.0).astype(BF16)

    def head_norm(values):
        high, low = halves(values * values)
        return values * lax.rsqrt(dot(high, head_mean) + dot(low, head_mean) + 1e-06)

    near_kv[0:rows, 0:width] = head_norm(project(1)).astype(BF16)
    near_kv[0:rows, width:] = project(2).astype(BF16)
    lower, upper = pl.ds(rows, WINDOW), pl.ds(rows + WINDOW, WINDOW)

    def halo(k, source, target, device):
        return pltpu.make_async_remote_copy(
            src_ref=near_kv.at[source], dst_ref=near_kv.at[target], send_sem=mem_send.at[k], recv_sem=mem_recv.at[k],
            device_id={"grid": device}, device_id_type=MESH,
        )

    to_next = halo(LOW, pl.ds(rows - WINDOW, WINDOW), lower, up_next)
    to_last = halo(HIGH, pl.ds(0, WINDOW), upper, down_next)
    to_next.start()
    to_last.start()

    n_heads = width // head_dim
    query = head_norm(project(0)).astype(BF16) * jnp.asarray(head_dim**-0.5, BF16)
    head_lane = lax.broadcasted_iota(jnp.int32, (rows, width), 1) // head_dim
    zero = jnp.zeros_like(query)
    heads = jnp.concatenate([jnp.where(head_lane == h, query, zero) for h in range(n_heads)], axis=0)
    tall = n_heads * rows
    q_pos = lax.rem(lax.broadcasted_iota(jnp.int32, (tall, rows), 0), rows)
    k_pos = lax.broadcasted_iota(jnp.int32, (tall, rows), 1)
    own_scores = dot_nt(heads, near_kv[0:rows, 0:width])
    own_exp = jnp.where(jnp.abs(q_pos - k_pos) <= WINDOW, jnp.exp(own_scores), 0.0)
    with jax.named_scope("w_halo"):
        to_next.wait()
        to_last.wait()
    far_pos = jnp.where(k_pos < WINDOW, k_pos - WINDOW, k_pos + rows - WINDOW)
    low_pos = jnp.where(me == 0, 0, -WINDOW)
    high_pos = jnp.where(me == n_grid - 1, rows, rows + WINDOW)
    far_ok = (jnp.abs(q_pos - far_pos) <= WINDOW) & (far_pos >= low_pos) & (far_pos < high_pos)
    far_exp = jnp.where(far_ok, jnp.exp(dot_nt(heads, near_kv[rows:, 0:width])), 0.0)
    total = jnp.sum(own_exp, axis=-1, keepdims=True) + jnp.sum(far_exp, axis=-1, keepdims=True)
    mixed = dot((own_exp / total).astype(BF16), near_kv[0:rows, width:])
    mixed += dot((far_exp / total).astype(BF16), near_kv[rows:, width:])
    joined = mixed[0:rows]
    for h in range(1, n_heads):
        joined = jnp.where(head_lane == h, mixed[h * rows : (h + 1) * rows], joined)
    attended[band] = joined.astype(BF16)
    gather_start(ATT, attended.at[band])

    out_half = out_v.shape[2] // 2
    for k, q in enumerate(beside[: n_band // 2]):
        with jax.named_scope(f"w_out{q}"):
            x_wait(OUT, q, out_v.at[bands[q], mem])
        if n_band > 2:
            piece = out_v.at[bands[q], mem, pl.ds(k * out_half, out_half)]
            start(x_copy(PASS, n_band - q, piece, piece))
        start(mem_copy(OUT_OWN + q, out_v.at[bands[q], mem]))
    for q in near_bands:
        with jax.named_scope(f"w_dec{q}"):
            x_wait(DEC, q, dec_v.at[bands[q], mem])
        start(mem_copy(DEC_OWN + q, dec_v.at[bands[q], mem]))

    half_cols = out_v.shape[3]
    with jax.named_scope("w_outown"):
        mem_copy(OUT_OWN, out_v.at[band, other]).wait_recv()
    sums = [dot(attended[band], out_v[band, m]).astype(BF16).astype(F32) for m in range(2)]
    if n_band > 2:
        with jax.named_scope("w_pass"):
            for k, q in enumerate(beside):
                x_wait(PASS, q, out_v.at[bands[across], mem, pl.ds(k * out_half, out_half)])
        start(mem_copy(OUT_OWN + across, out_v.at[bands[across], mem]))

    with jax.named_scope("w_down"):
        mem_copy(DOWN, down_v.at[other]).wait_recv()
    for q in near_bands:
        with jax.named_scope(f"w_decmem{q}"):
            mem_copy(DEC_OWN + q, dec_v.at[bands[q], other]).wait_recv()
    fold = 0.0
    for k in range(n_band):
        per_half = half_cols // width
        columns = slice((k % per_half) * width, (k % per_half + 1) * width)
        fold += dot(down_v[k // per_half, :, columns], dec_v[k].reshape(width, -1))
    high, low = halves(fold)
    fold_v[0] = high
    fold_v[1] = low

    for q in near_bands:
        with jax.named_scope(f"w_att{q}"):
            x_wait(ATT, q, attended.at[bands[q]])
        with jax.named_scope(f"w_outmem{q}"):
            mem_copy(OUT_OWN + q, out_v.at[bands[q], other]).wait_recv()
        left = attended[bands[q]]
        for m in range(2):
            sums[m] = sums[m] + dot(left, out_v[bands[q], m]).astype(BF16).astype(F32)
    stream = stream_v[...] + jnp.concatenate(sums, axis=1)
    stream_v[...] = stream
    normed = rms_norm(stream).astype(BF16)

    with jax.named_scope("w_up"):
        mem_copy(UP, up_v.at[other]).wait_recv()
    deep = up_v.shape[1]
    hidden = gelu(dot(normed[:, :deep], up_v[0]) + dot(normed[:, deep:], up_v[1])).astype(BF16)
    high, low = halves(stream_v[:, pl.ds(pl.multiple_of(band * width, width), width)])
    own_dec = dec_v[band].reshape(width, -1)
    part = dot(hidden, fold_v[0]) + dot(hidden, fold_v[1]) + dot(high, own_dec) + dot(low, own_dec)
    proj[band] = part.astype(BF16)
    gather_start(PROJ, proj.at[band])
    z_sent(0, send_z, states)
    passed_on(states, STATES)
    for q in near_bands:
        with jax.named_scope(f"w_proj{q}"):
            x_wait(PROJ, q, proj.at[bands[q]])
        part = part + proj[bands[q]].astype(F32)
    nodes = part.astype(BF16)
    outgoing = dot_tn(select[0, 0:rows], nodes) + dot_tn(select[0, rows : 2 * rows], nodes)
    back_z[...] = outgoing.astype(BF16).reshape(back_z.shape)
    z_start(1, back_z, returned)
    for copy in sent:
        copy.wait_send()

    with jax.named_scope("w_back"):
        for p in range(per):
            z_wait(1, p, back_z, returned)
            pass_on(p, returned, BACKS)
    decoded = dot(pick[0], returned[0].reshape(group, -1))
    for q in near_bands:
        with jax.named_scope(f"w_xb{q}"):
            for k in range(2):
                x_wait(BACKS[k], q, returned.at[q, parts[k]])
        decoded += dot(pick[q], returned[q].reshape(group, -1))
    result = jnp.where(free_v[...] > 0.5, grid_v[...].astype(F32) + decoded, forcing_v[...].astype(F32))
    next_ref[...] = result.astype(BF16)
    z_sent(1, back_z, returned)
    passed_on(returned, BACKS)


def body(
    grid_state, forcing, boundary_mask, edge_src, edge_dst, edge_count, edge_weight,
    embed_weight, attn_qkv, attn_out, mlp_in, mlp_out, decode_weight,
):
    n_grid, n_band, n_mem = lax.axis_size("grid"), lax.axis_size("band"), lax.axis_size("mem")
    grid_rows = grid_state[0]
    points, channels = grid_rows.shape
    slots = edge_src.shape[2]
    model = decode_weight.shape[0] * n_band
    width = embed_weight.shape[1]
    rows = M_DEV
    per = n_grid // n_band
    group = per * slots
    operands = (
        grid_rows, forcing, boundary_mask.reshape(-1, channels), edge_src[0], edge_dst, edge_count.T, edge_weight, embed_weight,
        jnp.swapaxes(attn_qkv[0], 0, 1), attn_out[0], mlp_in[0], mlp_out[0], decode_weight,
    )
    vmem = pltpu.VMEM
    spread_over = {7: (n_band,), 8: (n_mem,), 9: (n_band, n_mem), 10: (n_mem,), 11: (n_mem,)}
    scratch = [vmem((*spread_over.get(k, ()), *a.shape), a.dtype) for k, a in enumerate(operands[:12])]
    scratch += [
        vmem((n_band, n_mem, width // n_mem, channels), BF16),
        vmem((n_band, points, group), BF16),
        vmem((n_band, 2 * rows, group), BF16),
        vmem((points, channels), F32),
        vmem((per, slots, channels), BF16),
        vmem((n_band, per, slots, channels), BF16),
        vmem((rows + 2 * WINDOW, 2 * width), BF16),
        vmem((n_band, rows, width), BF16),
        vmem((rows, model), F32),
        vmem((2, mlp_out.shape[1], channels), BF16),
        vmem((n_band, rows, channels), BF16),
        vmem((per, slots, channels), BF16),
        vmem((n_band, per, slots, channels), BF16),
        pltpu.SemaphoreType.DMA((14,)),
        pltpu.SemaphoreType.DMA((2, per)),
        pltpu.SemaphoreType.DMA((2, per)),
        pltpu.SemaphoreType.DMA((len(STAGES), n_band)),
        pltpu.SemaphoreType.DMA((len(STAGES), n_band)),
        pltpu.SemaphoreType.DMA((2 * n_band + 5,)),
        pltpu.SemaphoreType.DMA((2 * n_band + 5,)),
    ]
    result = pl.pallas_call(
        functools.partial(step_kernel, n_grid, n_band, model // HEADS),
        out_shape=jax.ShapeDtypeStruct((points, channels), BF16),
        in_specs=[pl.BlockSpec(memory_space=pl.ANY)] * len(operands),
        out_specs=pl.BlockSpec(memory_space=pltpu.VMEM),
        scratch_shapes=scratch,
        compiler_params=pltpu.CompilerParams(collective_id=0, has_side_effects=True),
    )(*operands)
    return result[None]


def solution(mesh):
    return jax.shard_map(
        body,
        mesh=mesh,
        in_specs=(
            P(("dom", "mem"), "grid", None),
            P(("dom", "grid"), None),
            P("grid"),
            P("grid", None, None),
            P(None, "grid", None),
            P(None, "grid"),
            P(None, "grid", None),
            P(None, "band"),
            P(None, "mem", None, "band"),
            P(None, "band", "mem"),
            P(None, "mem", "band"),
            P(None, "band", "mem"),
            P("band", None),
        ),
        out_specs=P(("dom", "mem"), "grid", None),
        check_vma=False,
    )
```

time: 114 us -> 105 us (0.921)
  Pallas kernels: 112 us -> 103 us
  other arithmetic: 1.75 us -> 0 us
    pallas_call x1, Pallas kernels: 112 us -> 103 us  [body(): pl.pallas_call(functools.partial(step_kernel, n_grid, n_band, model // HE...]
    broadcast_in_dim x1 -> x0, other arithmetic: 1.74 us -> none  [body(): return result.astype(BF16)[None]]
where the time goes in v2:
time: 105 us
  Pallas kernels  103 us (98%)
  local copies, waits for them, and re-layouts  1.57 us (1%)
    pallas_call x1, Pallas kernels, body(): pl.pallas_call(functools.partial(step_kernel, n_grid, n_band, model // HE...  103 us

profile of v2, /device:TPU:40, one launch (start us, length us, event | category | flops | bytes accessed | tf_op | source)
XLA Modules:
  0.0 104.6 jit_solution(2369932858308674992)
XLA Ops:
  0.0 103.0 %shard_map.127 = bf16[512,128]{1,0:T(8,128)(2,1)} custom-call(bf16[512,128]{1,0:T(8,128)(2,1)} %bitcast.16, bf16[512,128]{1,0:T(8,128)(2,1)} %forcing_in.1, s32[4,128]{1,0:T(4,128)} %bitcast.18, s32[32,32]{1,0:T(8,128)} %bitcast.17, s32[32,1,32]{2,1,0:T(1,128)} %dst_in.1, s32[1,32]{1,0:T(1,128)} %bitcast.19, f32[32,1,32]{2,1,0:T(1,128)} %weight_in.1, ...), custom_call_target="tpu_custom_call" | custom-call | tf_op jit(solution)/shard_map/pallas_call | solution.py:495
  103.0 1.6 %copy.15 = bf16[1,512,128]{2,1,0:T(8,128)(2,1)} copy(bf16[1,512,128]{2,1,0:T(8,128)(2,1)} %bitcast.14) | data formatting | bytes 262144

commit v3 on v2

--- a/solution.py
+++ b/solution.py
@@ -35,7 +35,9 @@
 
 
 def gelu(x):
-    return 0.5 * x * (1.0 + jnp.tanh(math.sqrt(2.0 / math.pi) * (x + 0.044715 * (x * x * x))))
+    scale = math.sqrt(2.0 / math.pi)
+    half = 0.5 * x
+    return half * jnp.tanh(x * (x * x * (0.044715 * scale) + scale)) + half
 
 
 def rms_norm(values):
@@ -45,10 +47,6 @@
 def halves(values):
     high = values.astype(BF16)
     return high, (values - high.astype(F32)).astype(BF16)
-
-
-def near_first(count, stride, ring):
-    return sorted(range(count), key=lambda r: min(stride * r + stride // 2, ring - stride * r - stride // 2))
 
 
 def step_kernel(
@@ -56,8 +54,8 @@
     grid_in, forcing_in, mask_in, src_in, dst_in, count_in, weight_in, embed_in, qkv_in, out_in, up_in, down_in, dec_in,
     next_ref,
     grid_v, forcing_v, mask_v, src_v, dst_v, count_v, weight_v, embed_v, qkv_v, out_v, up_v, down_v, dec_v,
-    pick, select, free_v, send_z, states, near_kv, attended, stream_v, fold_v, proj, back_z, returned,
-    load_sem, z_send, z_recv, x_send, x_recv, mem_send, mem_recv,
+    pick, select, free_v, send_z, relayed, states, near_kv, attended, stream_v, fold_v, proj, back_z, returned,
+    load_sem, z_send, z_recv, hop_send, hop_recv, x_send, x_recv, mem_send, mem_recv,
 ):
     me = lax.axis_index("grid")
     band = lax.axis_index("band")
@@ -71,30 +69,34 @@
     far_bands = sorted(range(1, n_band), key=lambda q: -min(q, n_band - q))
     near_bands = far_bands[::-1]
     beside, across = (1, n_band - 1), n_band // 2
-    order = near_first(per, n_band, n_grid)
-    place_of = {r: p for p, r in enumerate(order)}
-    near = [lax.rem(bands[q] + 2 * (n_grid - me), n_band) for q in range(n_band)]
-    is_self = near[0] == 0
-
-    def z_peer(p):
-        return lax.rem(me + near[0] + n_band * order[p], n_grid)
-
-    def place_there(p):
-        r = order[p]
-        return jnp.where(is_self, place_of[(per - r) % per], place_of[per - 1 - r])
+    quarter, half_per = per // 4, per // 2
+    order = [*range(quarter), *range(3 * quarter, per), *range(quarter, 3 * quarter)]
+    ahead = [lax.rem(bands[q] + 2 * (n_grid - me), n_band) for q in range(n_band)]
+    behind = [lax.rem(n_band - a, n_band) for a in ahead]
+    is_self = ahead[0] == 0
+    reach = n_grid // 4
+    hops = (lax.rem(me + reach, n_grid), lax.rem(me + n_grid - reach, n_grid))
+
+    def ahead_at(r):
+        return lax.rem(me + ahead[0] + n_band * r, n_grid)
+
+    def behind_at(r):
+        return lax.rem(me + 2 * n_grid - behind[0] - n_band * r, n_grid)
 
     barrier = pltpu.get_barrier_semaphore()
 
     def greet(device):
         pl.semaphore_signal(barrier, inc=1, device_id=device, device_id_type=MESH)
 
-    for p in range(per)[::-1]:
+    for p in range(half_per)[::-1]:
         if order[p] == 0:
             @pl.when(jnp.logical_not(is_self))
             def _():
-                greet({"grid": z_peer(p)})
+                greet({"grid": ahead_at(0)})
         else:
-            greet({"grid": z_peer(p)})
+            greet({"grid": ahead_at(order[p])})
+    for device in hops:
+        greet({"grid": device})
     greet({"grid": up_next})
     greet({"grid": down_next})
     for q in far_bands:
@@ -116,81 +118,88 @@
     for load in loads:
         load.start()
 
-    lane = lax.broadcasted_iota(jnp.int32, (slots, group), 1)
-    spread = jnp.where(lax.rem(lane, slots) == lax.broadcasted_iota(jnp.int32, (slots, group), 0), 1.0, 0.0).astype(F32)
-    shard_row = lax.broadcasted_iota(jnp.int32, (n_grid, group), 0)
-    place_lane = lax.broadcasted_iota(jnp.int32, (n_grid, group), 1) // slots
-    step_lane = jnp.zeros_like(place_lane)
-    for p in range(per):
-        step_lane = jnp.where(place_lane == p, n_band * order[p], step_lane)
-
-    def lane_row(wide, q):
-        mine = shard_row == lax.rem(step_lane + (me + near[q]), n_grid)
+    span = half_per * slots
+    lane = lax.broadcasted_iota(jnp.int32, (slots, span), 1)
+    spread = jnp.where(lax.rem(lane, slots) == lax.broadcasted_iota(jnp.int32, (slots, span), 0), 1.0, 0.0).astype(F32)
+    shard_row = lax.broadcasted_iota(jnp.int32, (n_grid, span), 0)
+    place_lane = lax.broadcasted_iota(jnp.int32, (n_grid, span), 1) // slots
+    step_lane = []
+    for k in range(2):
+        steps = jnp.zeros_like(place_lane)
+        for p in range(half_per):
+            steps = jnp.where(place_lane == p, n_band * order[k * half_per + p], steps)
+        step_lane.append(steps)
+
+    def lane_row(wide, shards):
+        mine = shard_row == lax.rem(shards, n_grid)
         return jnp.sum(jnp.where(mine, wide, 0.0), axis=0, keepdims=True)
 
-    def build_pick(q):
-        point = lax.broadcasted_iota(jnp.int32, (grid_v.shape[0], group), 0).astype(F32)
-        pick[q] = jnp.where(point == lane_row(src_wide, q), 1.0, 0.0).astype(BF16)
+    point = lax.broadcasted_iota(jnp.int32, (grid_v.shape[0], span), 0).astype(F32)
+
+    def build_pick(k, q):
+        row = lane_row(src_wide, me + ahead[q] + step_lane[k])
+        pick[k, :, q * span : (q + 1) * span] = jnp.where(point == row, 1.0, 0.0).astype(BF16)
 
     with jax.named_scope("w_load"):
         loads[0].wait()
         loads[1].wait()
     src_wide = exact_dot(src_v[...].astype(F32), spread)
-    build_pick(0)
-    send_z[...] = dot_tn(pick[0], grid_v[...]).astype(BF16).reshape(send_z.shape)
+    for k in range(2):
+        build_pick(k, 0)
+        send_z[k] = dot_tn(pick[k, :, 0:span], grid_v[...]).astype(BF16).reshape(send_z.shape[1:])
 
     with jax.named_scope("w_barrier"):
-        pl.semaphore_wait(barrier, per + 2 + n_band - jnp.where(is_self, 1, 0))
-
-    def z_copy(way, p, source, target):
-        there = place_there(p)
+        pl.semaphore_wait(barrier, half_per + 4 + n_band - jnp.where(is_self, 1, 0))
+
+    def at_place(ref, p):
+        return ref.at[p // half_per, 0, p % half_per]
+
+    def z_copy(way, p, source, target, device):
         return pltpu.make_async_remote_copy(
-            src_ref=source.at[p], dst_ref=target.at[0, there], send_sem=z_send.at[way, p], recv_sem=z_recv.at[way, there],
-            device_id={"grid": z_peer(p)}, device_id_type=MESH,
-        )
-
-    def z_arrival(way, p, source, target):
-        return pltpu.make_async_remote_copy(
-            src_ref=source.at[p], dst_ref=target.at[0, p], send_sem=z_send.at[way, p], recv_sem=z_recv.at[way, p],
-            device_id={"grid": z_peer(p)}, device_id_type=MESH,
+            src_ref=source, dst_ref=at_place(target, p), send_sem=z_send.at[way, p], recv_sem=z_recv.at[way, p],
+            device_id={"grid": device}, device_id_type=MESH,
         )
 
     def z_own(way, p, source, target):
-        return pltpu.make_async_copy(source.at[p], target.at[0, p], z_recv.at[way, p])
-
-    def z_start(way, source, target):
-        for p in range(per)[::-1]:
-            if order[p] == 0:
+        return pltpu.make_async_copy(source, at_place(target, p), z_recv.at[way, p])
+
+    def may_stay(way, p):
+        return order[p] == 0 or (way == 0 and order[p] == quarter)
+
+    def each_way(way, p, stay, go):
+        if may_stay(way, p):
+            if stay is not None:
                 @pl.when(is_self)
                 def _():
-                    z_own(way, p, source, target).start()
-
-                @pl.when(jnp.logical_not(is_self))
-                def _():
-                    z_copy(way, p, source, target).start()
-            else:
-                z_copy(way, p, source, target).start()
-
-    def z_wait(way, p, source, target):
-        if order[p] == 0:
-            @pl.when(is_self)
-            def _():
-                z_own(way, p, source, target).wait()
+                    stay()
 
             @pl.when(jnp.logical_not(is_self))
             def _():
-                z_arrival(way, p, source, target).wait_recv()
+                go()
         else:
-            z_arrival(way, p, source, target).wait_recv()
-
-    def z_sent(way, source, target):
+            go()
+
+    def z_start(way, p, source, target, device):
+        each_way(
+            way, p, lambda: z_own(way, p, source, target).start(), lambda: z_copy(way, p, source, target, device).start()
+        )
+
+    def z_wait(way, p, target):
+        here = at_place(target, p)
+        each_way(
+            way, p, lambda: z_own(way, p, here, target).wait(), lambda: z_copy(way, p, here, target, up_next).wait_recv()
+        )
+
+    def z_sent(way, target):
         for p in range(per):
-            if order[p] == 0:
-                @pl.when(jnp.logical_not(is_self))
-                def _():
-                    z_copy(way, p, source, target).wait_send()
-            else:
-                z_copy(way, p, source, target).wait_send()
+            here = at_place(target, p)
+            each_way(way, p, None, lambda: z_copy(way, p, here, target, up_next).wait_send())
+
+    def hop_copy(k):
+        return pltpu.make_async_remote_copy(
+            src_ref=send_z.at[1, pl.ds(k * quarter, quarter)], dst_ref=relayed.at[k],
+            send_sem=hop_send.at[k], recv_sem=hop_recv.at[k], device_id={"grid": hops[k]}, device_id_type=MESH,
+        )
 
     def x_copy(stage, q, source, target):
         return pltpu.make_async_remote_copy(
@@ -222,16 +231,23 @@
 
     QKV, UP, DOWN, OUT_OWN, DEC_OWN, LOW, HIGH = 0, 1, 2, 3, 3 + n_band, 3 + 2 * n_band, 4 + 2 * n_band
 
-    z_start(0, send_z, states)
+    for k in range(2):
+        hop_copy(k).start()
+    for p in range(half_per)[::-1]:
+        z_start(0, p, send_z.at[0, p], states, ahead_at(order[p]))
     with jax.named_scope("w_load2"):
         loads[2].wait()
     gather_start(EMBED, embed_v.at[band])
     with jax.named_scope("w_load3"):
         for load in loads[3:]:
             load.wait()
-    for k, ref in ((QKV, qkv_v), (UP, up_v), (DOWN, down_v)):
+    for k, ref in ((QKV, qkv_v), (DOWN, down_v), (UP, up_v)):
         start(mem_copy(k, ref.at[mem]))
     start(mem_copy(OUT_OWN, out_v.at[band, mem]))
+    for q in far_bands:
+        start(x_copy(DEC, q, dec_v.at[band, mem], dec_v.at[band, mem]))
+    for q in beside[: n_band // 2]:
+        start(x_copy(OUT, q, out_v.at[band, mem], out_v.at[band, mem]))
 
     rows = stream_v.shape[0]
     square_row = lax.broadcasted_iota(jnp.int32, (n_grid, n_grid), 0)
@@ -241,14 +257,20 @@
     live = jnp.where(slot_lane < counts, weight_v[:, 0, :], 0.0)
     dst_wide = exact_dot(dst_v[:, 0, :].astype(F32), spread)
     live_wide = exact_dot(live, spread)
-    node = lax.broadcasted_iota(jnp.int32, (rows, group), 0).astype(F32)
-    for q in range(n_band):
-        table = jnp.where(node == lane_row(dst_wide, q), lane_row(live_wide, q), 0.0)
-        high, low = halves(table)
-        select[q, 0:rows] = high
-        select[q, rows : 2 * rows] = low
-    for q in range(1, n_band):
-        build_pick(q)
+    node = lax.broadcasted_iota(jnp.int32, (rows, span), 0).astype(F32)
+
+    def build_tables(k):
+        for q in range(n_band):
+            shards = me + 2 * n_grid - behind[q] - step_lane[k]
+            table = jnp.where(node == lane_row(dst_wide, shards), lane_row(live_wide, shards), 0.0)
+            high, low = halves(table)
+            select[k, 0:rows, q * span : (q + 1) * span] = high
+            select[k, rows : 2 * rows, q * span : (q + 1) * span] = low
+            if q:
+                build_pick(k, q)
+
+    build_tables(0)
+    build_tables(1)
     lanes = mask_v.shape[1]
     diagonal = lax.broadcasted_iota(jnp.int32, (lanes, lanes), 0) == lax.broadcasted_iota(jnp.int32, (lanes, lanes), 1)
     for k in range(mask_v.shape[0]):
@@ -256,24 +278,25 @@
         column = jnp.sum(jnp.where(diagonal, flags, 0.0), axis=1, keepdims=True)
         free_v[k * lanes : (k + 1) * lanes] = jnp.broadcast_to(column, (lanes, free_v.shape[1]))
 
-    near_part = per // 2
-    parts = (slice(0, near_part), slice(near_part, per))
+    with jax.named_scope("w_hop"):
+        for k in range(2):
+            hop_copy(k).wait_recv()
+            for t in range(quarter):
+                z_start(0, half_per + k * quarter + t, relayed.at[k, t], states, ahead_at((0, 3 * quarter)[k] + t))
 
     def pass_on(p, ref, stages):
+        k, t = p // half_per, p % half_per
         for q in far_bands:
-            x_copy(stages[p // near_part], q, ref.at[0, p], ref.at[n_band - q, p]).start()
+            x_copy(stages[k], q, ref.at[k, 0, t], ref.at[k, n_band - q, t]).start()
 
     def passed_on(ref, stages):
-        for k, part in enumerate(parts):
+        for k in range(2):
             for q in far_bands:
-                x_copy(stages[k], q, ref.at[0, part], ref.at[n_band - q, part]).wait_send()
+                x_copy(stages[k], q, ref.at[k, 0], ref.at[k, n_band - q]).wait_send()
 
     width = embed_v.shape[2]
 
-    def encode(k, q, first):
-        span = near_part * slots
-        block = states[q, parts[k]].reshape(span, -1)
-        table = select[q, :, k * span : (k + 1) * span]
+    def encode(block, table, first=False):
         for col in range(n_band):
             both = dot(table, gelu(dot(block, embed_v[col])).astype(BF16))
             part = both[:rows] + both[rows:]
@@ -281,27 +304,53 @@
             stream_v[:, cols] = part if first else stream_v[:, cols] + part
 
     with jax.named_scope("w_znear"):
-        for p in range(near_part):
-            z_wait(0, p, send_z, states)
+        for p in range(half_per):
+            z_wait(0, p, states)
             pass_on(p, states, STATES)
+    with jax.named_scope("w_zfar"):
+        for p in range(half_per, per):
+            z_wait(0, p, states)
+            pass_on(p, states, STATES)
+    out_half = out_v.shape[2] // 2
+    with jax.named_scope("w_dec"):
+        for q in near_bands:
+            x_wait(DEC, q, dec_v.at[bands[q], mem])
+            start(mem_copy(DEC_OWN + q, dec_v.at[bands[q], mem]))
+    with jax.named_scope("w_out"):
+        for k, q in enumerate(beside[: n_band // 2]):
+            x_wait(OUT, q, out_v.at[bands[q], mem])
+            if n_band > 2:
+                piece = out_v.at[bands[q], mem, pl.ds(k * out_half, out_half)]
+                start(x_copy(PASS, n_band - q, piece, piece))
+            start(mem_copy(OUT_OWN + q, out_v.at[bands[q], mem]))
     with jax.named_scope("w_embed"):
         for q in near_bands:
             x_wait(EMBED, q, embed_v.at[bands[q]])
-    encode(0, 0, True)
-    with jax.named_scope("w_zfar"):
-        for p in range(near_part, per):
-            z_wait(0, p, send_z, states)
-            pass_on(p, states, STATES)
-    for q in far_bands:
-        start(x_copy(DEC, q, dec_v.at[band, mem], dec_v.at[band, mem]))
-    for q in beside:
-        start(x_copy(OUT, q, out_v.at[band, mem], out_v.at[band, mem]))
-    encode(1, 0, False)
-    for k in range(2):
+    own = jnp.concatenate([states[k, 0].reshape(span, -1) for k in range(2)], axis=0)
+    encode(own, jnp.concatenate([select[k, :, 0:span] for k in range(2)], axis=1), True)
+    with jax.named_scope("w_xnear"):
         for q in near_bands:
-            with jax.named_scope(f"w_x{k}{q}"):
-                x_wait(STATES[k], q, states.at[q, parts[k]])
-            encode(k, q, False)
+            x_wait(STATES[0], q, states.at[0, q])
+    encode(states[0, 1:].reshape((n_band - 1) * span, -1), select[0, :, span:])
+
+    half_cols = out_v.shape[3]
+    with jax.named_scope("w_down"):
+        mem_copy(DOWN, down_v.at[other]).wait_recv()
+        for q in near_bands:
+            mem_copy(DEC_OWN + q, dec_v.at[bands[q], other]).wait_recv()
+    fold = 0.0
+    for k in range(n_band):
+        per_half = half_cols // width
+        columns = slice((k % per_half) * width, (k % per_half + 1) * width)
+        fold += dot(down_v[k // per_half, :, columns], dec_v[k].reshape(width, -1))
+    high, low = halves(fold)
+    fold_v[0] = high
+    fold_v[1] = low
+
+    with jax.named_scope("w_xfar"):
+        for q in near_bands:
+            x_wait(STATES[1], q, states.at[1, q])
+    encode(states[1, 1:].reshape((n_band - 1) * span, -1), select[1, :, span:])
     stream = stream_v[...].astype(BF16).astype(F32)
     stream_v[...] = stream
     normed = rms_norm(stream).astype(BF16)
@@ -346,6 +395,11 @@
     k_pos = lax.broadcasted_iota(jnp.int32, (tall, rows), 1)
     own_scores = dot_nt(heads, near_kv[0:rows, 0:width])
     own_exp = jnp.where(jnp.abs(q_pos - k_pos) <= WINDOW, jnp.exp(own_scores), 0.0)
+    if n_band > 2:
+        with jax.named_scope("w_pass"):
+            for k, q in enumerate(beside):
+                x_wait(PASS, q, out_v.at[bands[across], mem, pl.ds(k * out_half, out_half)])
+        start(mem_copy(OUT_OWN + across, out_v.at[bands[across], mem]))
     with jax.named_scope("w_halo"):
         to_next.wait()
         to_last.wait()
@@ -363,43 +417,9 @@
     attended[band] = joined.astype(BF16)
     gather_start(ATT, attended.at[band])
 
-    out_half = out_v.shape[2] // 2
-    for k, q in enumerate(beside[: n_band // 2]):
-        with jax.named_scope(f"w_out{q}"):
-            x_wait(OUT, q, out_v.at[bands[q], mem])
-        if n_band > 2:
-            piece = out_v.at[bands[q], mem, pl.ds(k * out_half, out_half)]
-            start(x_copy(PASS, n_band - q, piece, piece))
-        start(mem_copy(OUT_OWN + q, out_v.at[bands[q], mem]))
-    for q in near_bands:
-        with jax.named_scope(f"w_dec{q}"):
-            x_wait(DEC, q, dec_v.at[bands[q], mem])
-        start(mem_copy(DEC_OWN + q, dec_v.at[bands[q], mem]))
-
-    half_cols = out_v.shape[3]
     with jax.named_scope("w_outown"):
         mem_copy(OUT_OWN, out_v.at[band, other]).wait_recv()
     sums = [dot(attended[band], out_v[band, m]).astype(BF16).astype(F32) for m in range(2)]
-    if n_band > 2:
-        with jax.named_scope("w_pass"):
-            for k, q in enumerate(beside):
-                x_wait(PASS, q, out_v.at[bands[across], mem, pl.ds(k * out_half, out_half)])
-        start(mem_copy(OUT_OWN + across, out_v.at[bands[across], mem]))
-
-    with jax.named_scope("w_down"):
-        mem_copy(DOWN, down_v.at[other]).wait_recv()
-    for q in near_bands:
-        with jax.named_scope(f"w_decmem{q}"):
-            mem_copy(DEC_OWN + q, dec_v.at[bands[q], other]).wait_recv()
-    fold = 0.0
-    for k in range(n_band):
-        per_half = half_cols // width
-        columns = slice((k % per_half) * width, (k % per_half + 1) * width)
-        fold += dot(down_v[k // per_half, :, columns], dec_v[k].reshape(width, -1))
-    high, low = halves(fold)
-    fold_v[0] = high
-    fold_v[1] = low
-
     for q in near_bands:
         with jax.named_scope(f"w_att{q}"):
             x_wait(ATT, q, attended.at[bands[q]])
@@ -421,32 +441,39 @@
     part = dot(hidden, fold_v[0]) + dot(hidden, fold_v[1]) + dot(high, own_dec) + dot(low, own_dec)
     proj[band] = part.astype(BF16)
     gather_start(PROJ, proj.at[band])
-    z_sent(0, send_z, states)
+    z_sent(0, states)
+    for k in range(2):
+        hop_copy(k).wait_send()
     passed_on(states, STATES)
     for q in near_bands:
         with jax.named_scope(f"w_proj{q}"):
             x_wait(PROJ, q, proj.at[bands[q]])
         part = part + proj[bands[q]].astype(F32)
     nodes = part.astype(BF16)
-    outgoing = dot_tn(select[0, 0:rows], nodes) + dot_tn(select[0, rows : 2 * rows], nodes)
-    back_z[...] = outgoing.astype(BF16).reshape(back_z.shape)
-    z_start(1, back_z, returned)
+    for k in (1, 0):
+        outgoing = dot_tn(select[k, 0:rows, 0:span], nodes) + dot_tn(select[k, rows : 2 * rows, 0:span], nodes)
+        back_z[k] = outgoing.astype(BF16).reshape(back_z.shape[1:])
+        for t in range(half_per):
+            p = k * half_per + t
+            z_start(1, p, back_z.at[k, t], returned, behind_at(order[p]))
     for copy in sent:
         copy.wait_send()
 
     with jax.named_scope("w_back"):
         for p in range(per):
-            z_wait(1, p, back_z, returned)
+            z_wait(1, p, returned)
             pass_on(p, returned, BACKS)
-    decoded = dot(pick[0], returned[0].reshape(group, -1))
-    for q in near_bands:
-        with jax.named_scope(f"w_xb{q}"):
-            for k in range(2):
-                x_wait(BACKS[k], q, returned.at[q, parts[k]])
-        decoded += dot(pick[q], returned[q].reshape(group, -1))
+    decoded = 0.0
+    for k in range(2):
+        decoded += dot(pick[k, :, 0:span], returned[k, 0].reshape(span, -1))
+    for k in range(2):
+        with jax.named_scope(f"w_xb{k}"):
+            for q in near_bands:
+                x_wait(BACKS[k], q, returned.at[k, q])
+        decoded += dot(pick[k, :, span:], returned[k, 1:].reshape((n_band - 1) * span, -1))
     result = jnp.where(free_v[...] > 0.5, grid_v[...].astype(F32) + decoded, forcing_v[...].astype(F32))
     next_ref[...] = result.astype(BF16)
-    z_sent(1, back_z, returned)
+    z_sent(1, returned)
     passed_on(returned, BACKS)
 
 
@@ -472,21 +499,24 @@
     scratch = [vmem((*spread_over.get(k, ()), *a.shape), a.dtype) for k, a in enumerate(operands[:12])]
     scratch += [
         vmem((n_band, n_mem, width // n_mem, channels), BF16),
-        vmem((n_band, points, group), BF16),
-        vmem((n_band, 2 * rows, group), BF16),
+        vmem((2, points, n_band * group // 2), BF16),
+        vmem((2, 2 * rows, n_band * group // 2), BF16),
         vmem((points, channels), F32),
-        vmem((per, slots, channels), BF16),
-        vmem((n_band, per, slots, channels), BF16),
+        vmem((2, per // 2, slots, channels), BF16),
+        vmem((2, per // 4, slots, channels), BF16),
+        vmem((2, n_band, per // 2, slots, channels), BF16),
         vmem((rows + 2 * WINDOW, 2 * width), BF16),
         vmem((n_band, rows, width), BF16),
         vmem((rows, model), F32),
         vmem((2, mlp_out.shape[1], channels), BF16),
         vmem((n_band, rows, channels), BF16),
-        vmem((per, slots, channels), BF16),
-        vmem((n_band, per, slots, channels), BF16),
+        vmem((2, per // 2, slots, channels), BF16),
+        vmem((2, n_band, per // 2, slots, channels), BF16),
         pltpu.SemaphoreType.DMA((14,)),
         pltpu.SemaphoreType.DMA((2, per)),
         pltpu.SemaphoreType.DMA((2, per)),
+        pltpu.SemaphoreType.DMA((2,)),
+        pltpu.SemaphoreType.DMA((2,)),
         pltpu.SemaphoreType.DMA((len(STAGES), n_band)),
         pltpu.SemaphoreType.DMA((len(STAGES), n_band)),
         pltpu.SemaphoreType.DMA((2 * n_band + 5,)),

time: 105 us -> 102 us (0.971)
  Pallas kernels: 103 us -> 101 us
    pallas_call x1, Pallas kernels: 103 us -> 101 us  [body(): pl.pallas_call(functools.partial(step_kernel, n_grid, n_band, model // HE...]
where the time goes in v3:
time: 102 us
  Pallas kernels  101 us (99%)
  local copies, waits for them, and re-layouts  1.57 us (2%)
    pallas_call x1, Pallas kernels, body(): pl.pallas_call(functools.partial(step_kernel, n_grid, n_band, model // HE...  101 us

profile of v3, /device:TPU:40, one launch (start us, length us, event | category | flops | bytes accessed | tf_op | source)
XLA Modules:
  0.0 102.2 jit_solution(16034594210893119029)
XLA Ops:
  0.0 100.7 %shard_map.127 = bf16[512,128]{1,0:T(8,128)(2,1)} custom-call(bf16[512,128]{1,0:T(8,128)(2,1)} %bitcast.16, bf16[512,128]{1,0:T(8,128)(2,1)} %forcing_in.1, s32[4,128]{1,0:T(4,128)} %bitcast.18, s32[32,32]{1,0:T(8,128)} %bitcast.17, s32[32,1,32]{2,1,0:T(1,128)} %dst_in.1, s32[1,32]{1,0:T(1,128)} %bitcast.19, f32[32,1,32]{2,1,0:T(1,128)} %weight_in.1, ...), custom_call_target="tpu_custom_call" | custom-call | tf_op jit(solution)/shard_map/pallas_call | solution.py:525
  100.7 1.6 %copy.15 = bf16[1,512,128]{2,1,0:T(8,128)(2,1)} copy(bf16[1,512,128]{2,1,0:T(8,128)(2,1)} %bitcast.14) | data formatting | bytes 262144

commit v4 on v3

--- a/solution.py
+++ b/solution.py
@@ -11,6 +11,7 @@
 HEADS = 16
 M_DEV = 128
 WINDOW = 64
+VMEM_BYTES = 61_500_000
 EMBED, OUT, PASS, DEC, ATT, PROJ, *MORE = STAGES = range(10)
 STATES, BACKS = MORE[:2], MORE[2:]
 F32 = jnp.float32
@@ -83,6 +84,21 @@
     def behind_at(r):
         return lax.rem(me + 2 * n_grid - behind[0] - n_band * r, n_grid)
 
+    half = dec_v.shape[2]
+    loads = [
+        pltpu.make_async_copy(source, target, load_sem.at[k])
+        for k, (source, target) in enumerate(
+            (
+                (src_in, src_v), (grid_in, grid_v), (embed_in, embed_v.at[band]),
+                (dst_in, dst_v), (count_in, count_v), (weight_in, weight_v), (mask_in, mask_v), (forcing_in, forcing_v),
+                (qkv_in, qkv_v.at[mem]), (out_in, out_v.at[band, mem]), (up_in, up_v.at[mem]), (down_in, down_v.at[mem]),
+                (dec_in.at[0:half], dec_v.at[band, 0]), (dec_in.at[half : 2 * half], dec_v.at[band, 1]),
+            )
+        )
+    ]
+    loads[0].start()
+    loads[1].start()
+
     barrier = pltpu.get_barrier_semaphore()
 
     def greet(device):
@@ -103,19 +119,7 @@
         greet({"band": bands[q]})
     greet({"mem": other})
 
-    half = dec_v.shape[2]
-    loads = [
-        pltpu.make_async_copy(source, target, load_sem.at[k])
-        for k, (source, target) in enumerate(
-            (
-                (src_in, src_v), (grid_in, grid_v), (embed_in, embed_v.at[band]),
-                (dst_in, dst_v), (count_in, count_v), (weight_in, weight_v), (mask_in, mask_v), (forcing_in, forcing_v),
-                (qkv_in, qkv_v.at[mem]), (out_in, out_v.at[band, mem]), (up_in, up_v.at[mem]), (down_in, down_v.at[mem]),
-                (dec_in.at[0:half], dec_v.at[band, 0]), (dec_in.at[half : 2 * half], dec_v.at[band, 1]),
-            )
-        )
-    ]
-    for load in loads:
+    for load in loads[2:]:
         load.start()
 
     span = half_per * slots
@@ -419,15 +423,16 @@
 
     with jax.named_scope("w_outown"):
         mem_copy(OUT_OWN, out_v.at[band, other]).wait_recv()
-    sums = [dot(attended[band], out_v[band, m]).astype(BF16).astype(F32) for m in range(2)]
-    for q in near_bands:
-        with jax.named_scope(f"w_att{q}"):
+    sums = [dot(attended[band], out_v[band, m]) for m in range(2)]
+    with jax.named_scope("w_outmem"):
+        for q in near_bands:
+            mem_copy(OUT_OWN + q, out_v.at[bands[q], other]).wait_recv()
+    with jax.named_scope("w_att"):
+        for q in near_bands:
             x_wait(ATT, q, attended.at[bands[q]])
-        with jax.named_scope(f"w_outmem{q}"):
-            mem_copy(OUT_OWN + q, out_v.at[bands[q], other]).wait_recv()
-        left = attended[bands[q]]
-        for m in range(2):
-            sums[m] = sums[m] + dot(left, out_v[bands[q], m]).astype(BF16).astype(F32)
+    for m in range(2):
+        for q in near_bands:
+            sums[m] = sums[m] + dot(attended[bands[q]], out_v[bands[q], m])
     stream = stream_v[...] + jnp.concatenate(sums, axis=1)
     stream_v[...] = stream
     normed = rms_norm(stream).astype(BF16)
@@ -524,11 +529,11 @@
     ]
     result = pl.pallas_call(
         functools.partial(step_kernel, n_grid, n_band, model // HEADS),
-        out_shape=jax.ShapeDtypeStruct((points, channels), BF16),
+        out_shape=pltpu.VMEM((points, channels), BF16),
         in_specs=[pl.BlockSpec(memory_space=pl.ANY)] * len(operands),
         out_specs=pl.BlockSpec(memory_space=pltpu.VMEM),
         scratch_shapes=scratch,
-        compiler_params=pltpu.CompilerParams(collective_id=0, has_side_effects=True),
+        compiler_params=pltpu.CompilerParams(collective_id=0, has_side_effects=True, vmem_limit_bytes=VMEM_BYTES),
     )(*operands)
     return result[None]
 

time: 102 us -> 101 us (level)
  no operation moved by 1% of the time
where the time goes in v4:
time: 101 us
  Pallas kernels  100 us (99%)
    pallas_call x1, Pallas kernels, body(): pl.pallas_call(functools.partial(step_kernel, n_grid, n_band, model // HE...  100 us

profile of v4, /device:TPU:40, one launch (start us, length us, event | category | flops | bytes accessed | tf_op | source)
XLA Modules:
  0.0 100.9 jit_solution(8958783534131618953)
XLA Ops:
  0.0 100.2 %shard_map.127 = bf16[512,128]{1,0:T(8,128)(2,1)S(1)} custom-call(bf16[512,128]{1,0:T(8,128)(2,1)} %bitcast.16, bf16[512,128]{1,0:T(8,128)(2,1)} %forcing_in.1, s32[4,128]{1,0:T(4,128)} %bitcast.18, s32[32,32]{1,0:T(8,128)} %bitcast.17, s32[32,1,32]{2,1,0:T(1,128)} %dst_in.1, s32[1,32]{1,0:T(1,128)} %bitcast.19, f32[32,1,32]{2,1,0:T(1,128)} %weight_in.1, ...), custom_call_target="tpu_custom_call" | custom-call | tf_op jit(solution)/shard_map/pallas_call | solution.py:530
  100.2 0.7 copy.15

commit v5 on v4

--- a/solution.py
+++ b/solution.py
@@ -12,8 +12,8 @@
 M_DEV = 128
 WINDOW = 64
 VMEM_BYTES = 61_500_000
-EMBED, OUT, PASS, DEC, ATT, PROJ, *MORE = STAGES = range(10)
-STATES, BACKS = MORE[:2], MORE[2:]
+EMBED, OUT, PASS, DEC, ATT, PROJ, *MORE = STAGES = range(12)
+STATES, BACKS, CROSSED = MORE[:2], MORE[2:4], MORE[4:]
 F32 = jnp.float32
 BF16 = jnp.bfloat16
 MESH = pl.DeviceIdType.MESH
@@ -233,7 +233,7 @@
         for q in far_bands:
             start(x_copy(stage, q, ref, ref))
 
-    QKV, UP, DOWN, OUT_OWN, DEC_OWN, LOW, HIGH = 0, 1, 2, 3, 3 + n_band, 3 + 2 * n_band, 4 + 2 * n_band
+    QKV, UP, DOWN, OUT_OWN, DEC_OWN, HALO, CROSS = 0, 1, 2, 3, 3 + n_band, 3 + 2 * n_band, 7 + 2 * n_band
 
     for k in range(2):
         hop_copy(k).start()
@@ -374,20 +374,27 @@
         high, low = halves(values * values)
         return values * lax.rsqrt(dot(high, head_mean) + dot(low, head_mean) + 1e-06)
 
+    lower, upper = pl.ds(rows, WINDOW), pl.ds(rows + WINDOW, WINDOW)
+    both_sides = ((pl.ds(rows - WINDOW, WINDOW), lower, up_next), (pl.ds(0, WINDOW), upper, down_next))
+
+    def halo(which):
+        lanes = pl.ds(which * width, width)
+        return [
+            pltpu.make_async_remote_copy(
+                src_ref=near_kv.at[source, lanes], dst_ref=near_kv.at[target, lanes],
+                send_sem=mem_send.at[HALO + 2 * which + k], recv_sem=mem_recv.at[HALO + 2 * which + k],
+                device_id={"grid": device}, device_id_type=MESH,
+            )
+            for k, (source, target, device) in enumerate(both_sides)
+        ]
+
     near_kv[0:rows, 0:width] = head_norm(project(1)).astype(BF16)
+    key_halo, value_halo = halo(0), halo(1)
+    for copy in key_halo:
+        copy.start()
     near_kv[0:rows, width:] = project(2).astype(BF16)
-    lower, upper = pl.ds(rows, WINDOW), pl.ds(rows + WINDOW, WINDOW)
-
-    def halo(k, source, target, device):
-        return pltpu.make_async_remote_copy(
-            src_ref=near_kv.at[source], dst_ref=near_kv.at[target], send_sem=mem_send.at[k], recv_sem=mem_recv.at[k],
-            device_id={"grid": device}, device_id_type=MESH,
-        )
-
-    to_next = halo(LOW, pl.ds(rows - WINDOW, WINDOW), lower, up_next)
-    to_last = halo(HIGH, pl.ds(0, WINDOW), upper, down_next)
-    to_next.start()
-    to_last.start()
+    for copy in value_halo:
+        copy.start()
 
     n_heads = width // head_dim
     query = head_norm(project(0)).astype(BF16) * jnp.asarray(head_dim**-0.5, BF16)
@@ -405,14 +412,17 @@
                 x_wait(PASS, q, out_v.at[bands[across], mem, pl.ds(k * out_half, out_half)])
         start(mem_copy(OUT_OWN + across, out_v.at[bands[across], mem]))
     with jax.named_scope("w_halo"):
-        to_next.wait()
-        to_last.wait()
+        for copy in key_halo:
+            copy.wait()
     far_pos = jnp.where(k_pos < WINDOW, k_pos - WINDOW, k_pos + rows - WINDOW)
     low_pos = jnp.where(me == 0, 0, -WINDOW)
     high_pos = jnp.where(me == n_grid - 1, rows, rows + WINDOW)
     far_ok = (jnp.abs(q_pos - far_pos) <= WINDOW) & (far_pos >= low_pos) & (far_pos < high_pos)
     far_exp = jnp.where(far_ok, jnp.exp(dot_nt(heads, near_kv[rows:, 0:width])), 0.0)
     total = jnp.sum(own_exp, axis=-1, keepdims=True) + jnp.sum(far_exp, axis=-1, keepdims=True)
+    with jax.named_scope("w_halo_v"):
+        for copy in value_halo:
+            copy.wait()
     mixed = dot((own_exp / total).astype(BF16), near_kv[0:rows, width:])
     mixed += dot((far_exp / total).astype(BF16), near_kv[rows:, width:])
     joined = mixed[0:rows]
@@ -455,19 +465,94 @@
             x_wait(PROJ, q, proj.at[bands[q]])
         part = part + proj[bands[q]].astype(F32)
     nodes = part.astype(BF16)
+
+    passing = mem == 1
+    stays = is_self & passing
+    guest = n_band
+
+    def back_copy(p, device):
+        k, t = p // half_per, p % half_per
+        return pltpu.make_async_remote_copy(
+            src_ref=back_z.at[k, t], dst_ref=returned.at[k, (1 - mem) * guest, t],
+            send_sem=z_send.at[1, p], recv_sem=z_recv.at[2 - mem, p],
+            device_id={"grid": device, "mem": 1}, device_id_type=MESH,
+        )
+
+    def back_own(p):
+        return pltpu.make_async_copy(back_z.at[0, p], returned.at[0, 0, p], z_recv.at[1, p])
+
+    def unless_own(p, go, stay=None):
+        if order[p] == 0:
+            if stay is not None:
+                pl.when(stays)(stay)
+            pl.when(jnp.logical_not(stays))(go)
+        else:
+            go()
+
+    def back_wait(p, slot):
+        k, t = p // half_per, p % half_per
+        return pltpu.make_async_remote_copy(
+            src_ref=back_z.at[k, t], dst_ref=returned.at[k, slot, t],
+            send_sem=z_send.at[1, p], recv_sem=z_recv.at[2 if slot else 1, p],
+            device_id={"grid": up_next}, device_id_type=MESH,
+        )
+
+    def guest_copies(p):
+        k, t = p // half_per, p % half_per
+        block = returned.at[k, guest, t]
+        copies = [
+            pltpu.make_async_remote_copy(
+                src_ref=block, dst_ref=returned.at[k, n_band - q, t],
+                send_sem=x_send.at[CROSSED[k], q], recv_sem=x_recv.at[BACKS[k], n_band - q],
+                device_id={"band": bands[q], "mem": 0}, device_id_type=MESH,
+            )
+            for q in far_bands
+        ]
+        return copies + [
+            pltpu.make_async_remote_copy(
+                src_ref=block, dst_ref=returned.at[k, 0, t],
+                send_sem=mem_send.at[CROSS + k], recv_sem=mem_recv.at[CROSS + k],
+                device_id={"mem": 0}, device_id_type=MESH,
+            )
+        ]
+
+    def guest_half(k, q):
+        whole = returned.at[k, guest]
+        if q:
+            return pltpu.make_async_remote_copy(
+                src_ref=whole, dst_ref=returned.at[k, n_band - q],
+                send_sem=x_send.at[CROSSED[k], q], recv_sem=x_recv.at[BACKS[k], n_band - q],
+                device_id={"band": bands[q], "mem": 0}, device_id_type=MESH,
+            )
+        return pltpu.make_async_remote_copy(
+            src_ref=whole, dst_ref=returned.at[k, 0], send_sem=mem_send.at[CROSS + k], recv_sem=mem_recv.at[CROSS + k],
+            device_id={"mem": 0}, device_id_type=MESH,
+        )
+
     for k in (1, 0):
         outgoing = dot_tn(select[k, 0:rows, 0:span], nodes) + dot_tn(select[k, rows : 2 * rows, 0:span], nodes)
         back_z[k] = outgoing.astype(BF16).reshape(back_z.shape[1:])
         for t in range(half_per):
             p = k * half_per + t
-            z_start(1, p, back_z.at[k, t], returned, behind_at(order[p]))
+            unless_own(p, lambda: back_copy(p, behind_at(order[p])).start(), lambda: back_own(p).start())
     for copy in sent:
         copy.wait_send()
 
-    with jax.named_scope("w_back"):
+    @pl.when(passing)
+    def _():
         for p in range(per):
-            z_wait(1, p, returned)
+            unless_own(p, lambda: back_wait(p, 0).wait_recv(), lambda: back_own(p).wait())
             pass_on(p, returned, BACKS)
+        for p in range(per):
+            back_wait(p, guest).wait_recv()
+            for copy in guest_copies(p):
+                copy.start()
+
+    @pl.when(jnp.logical_not(passing))
+    def _():
+        for k in range(2):
+            guest_half(k, 0).wait_recv()
+
     decoded = 0.0
     for k in range(2):
         decoded += dot(pick[k, :, 0:span], returned[k, 0].reshape(span, -1))
@@ -475,11 +560,18 @@
         with jax.named_scope(f"w_xb{k}"):
             for q in near_bands:
                 x_wait(BACKS[k], q, returned.at[k, q])
-        decoded += dot(pick[k, :, span:], returned[k, 1:].reshape((n_band - 1) * span, -1))
+        decoded += dot(pick[k, :, span:], returned[k, 1:n_band].reshape((n_band - 1) * span, -1))
     result = jnp.where(free_v[...] > 0.5, grid_v[...].astype(F32) + decoded, forcing_v[...].astype(F32))
     next_ref[...] = result.astype(BF16)
-    z_sent(1, returned)
-    passed_on(returned, BACKS)
+    for p in range(per):
+        unless_own(p, lambda: back_copy(p, behind_at(order[p])).wait_send())
+
+    @pl.when(passing)
+    def _():
+        passed_on(returned, BACKS)
+        for k in range(2):
+            for q in range(n_band):
+                guest_half(k, q).wait_send()
 
 
 def body(
@@ -516,16 +608,16 @@
         vmem((2, mlp_out.shape[1], channels), BF16),
         vmem((n_band, rows, channels), BF16),
         vmem((2, per // 2, slots, channels), BF16),
-        vmem((2, n_band, per // 2, slots, channels), BF16),
+        vmem((2, n_band + 1, per // 2, slots, channels), BF16),
         pltpu.SemaphoreType.DMA((14,)),
         pltpu.SemaphoreType.DMA((2, per)),
-        pltpu.SemaphoreType.DMA((2, per)),
+        pltpu.SemaphoreType.DMA((3, per)),
         pltpu.SemaphoreType.DMA((2,)),
         pltpu.SemaphoreType.DMA((2,)),
         pltpu.SemaphoreType.DMA((len(STAGES), n_band)),
         pltpu.SemaphoreType.DMA((len(STAGES), n_band)),
-        pltpu.SemaphoreType.DMA((2 * n_band + 5,)),
-        pltpu.SemaphoreType.DMA((2 * n_band + 5,)),
+        pltpu.SemaphoreType.DMA((2 * n_band + 9,)),
+        pltpu.SemaphoreType.DMA((2 * n_band + 9,)),
     ]
     result = pl.pallas_call(
         functools.partial(step_kernel, n_grid, n_band, model // HEADS),

time: 101 us -> 100 us (0.990)
  no operation moved by 1% of the time
where the time goes in v5:
time: 100 us
  Pallas kernels  99.5 us (100%)
    pallas_call x1, Pallas kernels, body(): pl.pallas_call(functools.partial(step_kernel, n_grid, n_band, model // HE...  99.5 us

profile of v5, /device:TPU:40, one launch (start us, length us, event | category | flops | bytes accessed | tf_op | source)
XLA Modules:
  0.0 100.1 jit_solution(12829315935178257555)
XLA Ops:
  0.0 99.5 %shard_map.127 = bf16[512,128]{1,0:T(8,128)(2,1)S(1)} custom-call(bf16[512,128]{1,0:T(8,128)(2,1)} %bitcast.16, bf16[512,128]{1,0:T(8,128)(2,1)} %forcing_in.1, s32[4,128]{1,0:T(4,128)} %bitcast.18, s32[32,32]{1,0:T(8,128)} %bitcast.17, s32[32,1,32]{2,1,0:T(1,128)} %dst_in.1, s32[1,32]{1,0:T(1,128)} %bitcast.19, f32[32,1,32]{2,1,0:T(1,128)} %weight_in.1, ...), custom_call_target="tpu_custom_call" | custom-call | tf_op jit(solution)/shard_map/pallas_call | solution.py:622
  99.5 0.7 copy.15

commit v6 on v5

--- a/solution.py
+++ b/solution.py
@@ -282,11 +282,21 @@
         column = jnp.sum(jnp.where(diagonal, flags, 0.0), axis=1, keepdims=True)
         free_v[k * lanes : (k + 1) * lanes] = jnp.broadcast_to(column, (lanes, free_v.shape[1]))
 
+    def forward(k):
+        hop_copy(k).wait_recv()
+        for t in range(quarter):
+            z_start(0, half_per + k * quarter + t, relayed.at[k, t], states, ahead_at((0, 3 * quarter)[k] + t))
+
     with jax.named_scope("w_hop"):
-        for k in range(2):
-            hop_copy(k).wait_recv()
-            for t in range(quarter):
-                z_start(0, half_per + k * quarter + t, relayed.at[k, t], states, ahead_at((0, 3 * quarter)[k] + t))
+        @pl.when(me < reach)
+        def _():
+            forward(1)
+            forward(0)
+
+        @pl.when(me >= reach)
+        def _():
+            forward(0)
+            forward(1)
 
     def pass_on(p, ref, stages):
         k, t = p // half_per, p % half_per

time: 100 us -> 100 us (level)
  no operation moved by 1% of the time
where the time goes in v6:
time: 100 us
  Pallas kernels  99.5 us (100%)
    pallas_call x1, Pallas kernels, body(): pl.pallas_call(functools.partial(step_kernel, n_grid, n_band, model // HE...  99.5 us

profile of v6, /device:TPU:40, one launch (start us, length us, event | category | flops | bytes accessed | tf_op | source)
XLA Modules:
  0.0 100.1 jit_solution(8289580374234139825)
XLA Ops:
  0.0 99.5 %shard_map.127 = bf16[512,128]{1,0:T(8,128)(2,1)S(1)} custom-call(bf16[512,128]{1,0:T(8,128)(2,1)} %bitcast.16, bf16[512,128]{1,0:T(8,128)(2,1)} %forcing_in.1, s32[4,128]{1,0:T(4,128)} %bitcast.18, s32[32,32]{1,0:T(8,128)} %bitcast.17, s32[32,1,32]{2,1,0:T(1,128)} %dst_in.1, s32[1,32]{1,0:T(1,128)} %bitcast.19, f32[32,1,32]{2,1,0:T(1,128)} %weight_in.1, ...), custom_call_target="tpu_custom_call" | custom-call | tf_op jit(solution)/shard_map/pallas_call | solution.py:632
  99.5 0.7 copy.15
